TPU v7x, 32 devices: a whole 2x2x4 slice. The times are simulated.
32 devices in a mesh: batch: 4 (over x, core), space: 8 (over z, y).
Axes of the slice: x: 2, y: 2, z: 4, core: 2. Of those that a mesh axis runs over, the one named last changes fastest.
Arguments:
- inputs: bfloat16 [4, 128, 64, 64, 128], P('batch', 'space'), may hold values from -6 to 6
- cotangent: bfloat16 [4, 128, 64, 64, 128], P('batch', 'space'), may hold values from -6 to 6
- mode_weights: bfloat16 [256, 16, 64, 128], P('space'), may hold values from -1.5 to 1.5
Outputs:
- input_grad: bfloat16 [4, 128, 64, 64, 128], P('batch', 'space')
- weight_grad: float32 [256, 16, 64, 128], P('space')
All inputs are finite; a program needn't handle non-finite values.
Results may differ from a plain program's by a relative error of at most 0.015.
Values may be sent and summed in bfloat16 or wider, within the bound.
No kernel may reach another device: no remote copies, remote signals or barrier semaphores. Data moves between devices by JAX's collectives and lax.ppermute only.
A program may use at most 192 MiB of HBM per device.

v0:
```python
import math

import jax
import jax.numpy as jnp
from jax import lax
from jax.sharding import PartitionSpec as P

C = 64
X = 64
Y = 128
Z = 128
MX = 16
MY = 16
MZ = 16


two_pi = 2.0 * math.pi
highest = lax.Precision.HIGHEST


def twiddles(wave_list, positions, length):
    product = wave_list[:, None] * positions[None, :] % length
    angles = two_pi / length * product.astype(jnp.float32)
    return (jnp.cos(angles), jnp.sin(angles))


def wave_pair(retained, length):
    return jnp.concatenate([jnp.arange(retained // 2), jnp.arange(length - retained // 2, length)])


def plane_spectrum(values, z_table, cos_x, sin_x, factor):
    lead_dims = values.shape[:-3]
    along_z = jnp.dot(values.reshape(-1, Z), z_table, preferred_element_type=jnp.float32)
    along_z = along_z.reshape(lead_dims + (C, X, 2 * MZ))
    first_term = jnp.einsum("kx,...cxm->...ckm", cos_x, along_z, precision=highest)
    second_term = jnp.einsum("kx,...cxm->...ckm", sin_x, along_z, precision=highest)
    real_part = (first_term[..., :MZ] + second_term[..., MZ:]) * factor
    imag_part = (first_term[..., MZ:] - second_term[..., :MZ]) * factor
    stacked = jnp.stack([real_part, imag_part], axis=-4)
    return stacked.reshape(lead_dims + (2, C, MX * MZ)).astype(jnp.bfloat16)


def modes_along_y(spectra, cos_y, sin_y):
    values_f = spectra.astype(jnp.float32)
    real_in = values_f[:, :, 0]
    imag_in = values_f[:, :, 1]
    real_out = jnp.einsum("ky,bycp->pbkc", cos_y, real_in, precision=highest) + jnp.einsum(
        "ky,bycp->pbkc", sin_y, imag_in, precision=highest
    )
    imag_out = jnp.einsum("ky,bycp->pbkc", cos_y, imag_in, precision=highest) - jnp.einsum(
        "ky,bycp->pbkc", sin_y, real_in, precision=highest
    )
    return jnp.stack([real_out, imag_out], axis=3)


def planes_along_y(mode_data, cos_y, sin_y):
    values_f = mode_data.astype(jnp.float32)
    real_in = values_f[:, :, :, 0]
    imag_in = values_f[:, :, :, 1]
    real_out = jnp.einsum("ky,pbkc->bycp", cos_y, real_in, precision=highest) - jnp.einsum(
        "ky,pbkc->bycp", sin_y, imag_in, precision=highest
    )
    imag_out = jnp.einsum("ky,pbkc->bycp", sin_y, real_in, precision=highest) + jnp.einsum(
        "ky,pbkc->bycp", cos_y, imag_in, precision=highest
    )
    return jnp.stack([real_out, imag_out], axis=2)


def plane_inverse(spectra, cos_x, sin_x, z_back):
    lead_dims = spectra.shape[:-3]
    values_f = spectra.astype(jnp.float32).reshape(lead_dims + (2, C, MX, MZ))
    real_in = values_f[..., 0, :, :, :]
    imag_in = values_f[..., 1, :, :, :]
    real_out = jnp.einsum("kx,...ckm->...cxm", cos_x, real_in, precision=highest) - jnp.einsum(
        "kx,...ckm->...cxm", sin_x, imag_in, precision=highest
    )
    imag_out = jnp.einsum("kx,...ckm->...cxm", sin_x, real_in, precision=highest) + jnp.einsum(
        "kx,...ckm->...cxm", cos_x, imag_in, precision=highest
    )
    joined = jnp.concatenate([real_out, imag_out], axis=-1)
    result = jnp.dot(
        joined.reshape(-1, 2 * MZ), z_back, precision=highest, preferred_element_type=jnp.float32
    )
    return result.reshape(lead_dims + (C, X, Z)).astype(jnp.bfloat16)


def split_cot(cot_modes):
    real_part = cot_modes[:, :, :, 0]
    imag_part = cot_modes[:, :, :, 1]
    return (
        jnp.concatenate([real_part, imag_part], axis=-1),
        jnp.concatenate([imag_part, -real_part], axis=-1),
    )


def weight_terms(input_modes, cot_modes):
    cot_one, cot_two = split_cot(cot_modes)
    first_term = jnp.einsum(
        "pbki,pbkj->pkij", input_modes[:, :, :, 0], cot_one, preferred_element_type=jnp.float32
    )
    second_term = jnp.einsum(
        "pbki,pbkj->pkij", input_modes[:, :, :, 1], cot_two, preferred_element_type=jnp.float32
    )
    return first_term + second_term


def local(inputs, cotangent, mode_weights):
    inv_scale = 1.0 / math.sqrt(X * Y * Z)
    cos_z, sin_z = twiddles(jnp.arange(MZ), jnp.arange(Z), Z)
    z_table = jnp.concatenate([cos_z.T, -sin_z.T], axis=1).astype(jnp.bfloat16)
    z_back = jnp.concatenate([cos_z, -sin_z], axis=0) * inv_scale
    cos_x, sin_x = twiddles(wave_pair(MX, X), jnp.arange(X), X)
    plain_z = jnp.full((MZ,), inv_scale, jnp.float32)
    weight_z = jnp.where(jnp.arange(MZ) == 0, 1.0, 2.0).astype(jnp.float32) * inv_scale
    input_spec = plane_spectrum(inputs, z_table, cos_x, sin_x, plain_z)
    cot_spec = plane_spectrum(cotangent, z_table, cos_x, sin_x, weight_z)
    y_waves = wave_pair(MY, Y)
    positions = jnp.arange(Y)
    cos_y, sin_y = twiddles(y_waves, positions, Y)
    moved_input, moved_cot = (
        lax.all_to_all(input_spec, "space", split_axis=4, concat_axis=1, tiled=True),
        lax.all_to_all(cot_spec, "space", split_axis=4, concat_axis=1, tiled=True),
    )
    input_modes = modes_along_y(moved_input, cos_y, sin_y)
    cot_modes = modes_along_y(moved_cot, cos_y, sin_y)
    input_modes = input_modes.astype(jnp.bfloat16)
    cot_modes = cot_modes.astype(jnp.bfloat16)
    weight_grad = lax.psum(
        weight_terms(input_modes, cot_modes).astype(jnp.bfloat16), "batch"
    ).astype(jnp.float32)
    cot_one, cot_two = split_cot(cot_modes)
    grad_real = jnp.einsum(
        "pbkj,pkij->pbki", cot_one, mode_weights, preferred_element_type=jnp.float32
    )
    grad_imag = jnp.einsum(
        "pbkj,pkij->pbki", cot_two, mode_weights, preferred_element_type=jnp.float32
    )
    mode_grad = jnp.stack([grad_real, grad_imag], axis=3).astype(jnp.bfloat16)
    plane_modes = planes_along_y(mode_grad, cos_y, sin_y).astype(jnp.bfloat16)
    back_spec = lax.all_to_all(plane_modes, "space", split_axis=1, concat_axis=4, tiled=True)
    input_grad = plane_inverse(back_spec, cos_x, sin_x, z_back)
    return (input_grad, weight_grad)


def solution(mesh):
    placed = (
        P("batch", "space", None, None, None),
        P("batch", "space", None, None, None),
        P("space", None, None, None),
    )
    return jax.shard_map(
        local,
        mesh=mesh,
        in_specs=placed,
        out_specs=(P("batch", "space", None, None, None), P("space", None, None, None)),
        check_vma=False,
    )
```

profile of v0, /device:TPU:0, one launch (start us, length us, event | category | flops | bytes accessed | tf_op | source)
XLA Modules:
  0.0 509.5 jit_solution(14194246704716014748)
XLA Ops:
  7.2 15.0 %convolution_bitcast_fusion.1 = f32[65536,32]{0,1:T(8,128)} fusion(bf16[65536,128]{1,0:T(8,128)(2,1)} %bitcast.208, bf16[128,16]{0,1:T(8,128)(2,1)S(1)} %get-tuple-element.24, bf16[128,16]{0,1:T(8,128)(2,1)S(1)} %get-tuple-element.25), kind=kOutput, calls=%fused_computation.1 | convolution fusion | flops 536887296 | bytes 25174016 | tf_op jit(solution)/shard_map/dot_general | solution.py:33
  22.3 12.2 %reshape.397 = f32[16,64,64,32]{2,1,0,3:T(8,128)} reshape(f32[65536,32]{0,1:T(8,128)} %convolution_bitcast_fusion.1) | data formatting | bytes 16777216 | tf_op jit(solution)/shard_map/reshape
  34.5 41.9 %fusion.15 = f32[1,16,64,16,32]{2,3,4,1,0:T(8,128)S(1)} fusion(f32[16,64,64,32]{2,1,0,3:T(8,128)} %reshape.397, s32[16]{0:T(128)S(1)} %get-tuple-element.21), kind=kOutput, calls=%fused_computation.18 | convolution fusion | flops 402667520 | bytes 10485824 | tf_op jit(solution)/shard_map/kx,...cxm->...ckm/dot_general | solution.py:36
  76.5 39.9 %fusion.12 = f32[1,16,64,16,32]{2,3,4,1,0:T(8,128)S(1)} fusion(f32[16,64,64,32]{2,1,0,3:T(8,128)S(1)} %copy-done, s32[16]{0:T(128)S(1)} %get-tuple-element.21), kind=kOutput, calls=%fused_computation.17 | convolution fusion | flops 402667520 | bytes 10485824 | tf_op jit(solution)/shard_map/kx,...cxm->...ckm/dot_general | solution.py:35
  119.7 2.7 reshape.424
  122.4 7.3 %all-to-all-start = ((bf16[8,2,32768]{2,1,0:T(2,128)(2,1)}), bf16[8,2,32768]{2,1,0:T(2,128)(2,1)S(1)}, u32[]{:S(2)}, u32[]{:S(2)}) async-start(bf16[8,2,32768]{2,1,0:T(2,128)(2,1)} %reshape.424), calls=%async_computation | async-start | bytes 2097152 | tf_op jit(solution)/shard_map/all_to_all | solution.py:122
  129.7 15.0 %convolution_bitcast_fusion = f32[65536,32]{0,1:T(8,128)} fusion(bf16[65536,128]{1,0:T(8,128)(2,1)} %bitcast.209, bf16[128,16]{0,1:T(8,128)(2,1)S(1)} %get-tuple-element.24, bf16[128,16]{0,1:T(8,128)(2,1)S(1)} %get-tuple-element.25), kind=kOutput, calls=%fused_computation | convolution fusion | flops 536887296 | bytes 25174016 | tf_op jit(solution)/shard_map/dot_general | solution.py:33
  144.7 12.2 %reshape.406 = f32[16,64,64,32]{2,1,0,3:T(8,128)} reshape(f32[65536,32]{0,1:T(8,128)} %convolution_bitcast_fusion) | data formatting | bytes 16777216 | tf_op jit(solution)/shard_map/reshape.48
  157.0 41.9 %fusion.21 = f32[1,16,64,16,32]{2,3,4,1,0:T(8,128)S(1)} fusion(f32[16,64,64,32]{2,1,0,3:T(8,128)} %reshape.406, s32[16]{0:T(128)S(1)} %get-tuple-element.21), kind=kOutput, calls=%fused_computation.20 | convolution fusion | flops 402667520 | bytes 10485824 | tf_op jit(solution)/shard_map/kx,...cxm->...ckm/dot_general | solution.py:36
  198.9 39.6 %fusion.18 = f32[1,16,64,16,32]{2,3,4,1,0:T(8,128)S(1)} fusion(f32[16,64,64,32]{2,1,0,3:T(8,128)S(1)} %copy-done.1, s32[16]{0:T(128)S(1)} %get-tuple-element.21), kind=kOutput, calls=%fused_computation.19 | convolution fusion | flops 402667520 | bytes 10485824 | tf_op jit(solution)/shard_map/kx,...cxm->...ckm/dot_general | solution.py:35
  241.7 2.6 reshape.428
  245.3 6.0 %all-to-all-start.2 = ((bf16[8,2,32768]{2,1,0:T(2,128)(2,1)}), bf16[8,2,32768]{2,1,0:T(2,128)(2,1)S(1)}, u32[]{:S(2)}, u32[]{:S(2)}) async-start(bf16[8,2,32768]{2,1,0:T(2,128)(2,1)} %reshape.428), calls=%async_computation.2 | async-start | bytes 2097152 | tf_op jit(solution)/shard_map/all_to_all | solution.py:121
  251.3 3.3 reshape.425
  258.0 3.6 copy.109
  261.6 3.6 copy.108
  265.2 3.3 fusion.59
  268.4 3.3 fusion.45
  274.5 7.8 %fusion.64 = f32[32,16,1,64]{3,2,1,0:T(1,128)S(1)} fusion(bf16[32,16,64,128]{3,2,1,0:T(8,128)(2,1)} %param.5, bf16[32,16,128,1]{2,1,0,3:T(8,128)(2,1)S(1)} %get-tuple-element.15), kind=kOutput, calls=%fused_computation.76 | convolution fusion | flops 8388608 | bytes 8650752 | tf_op jit(solution)/shard_map/pbkj,pkij->pbki/dot_general | solution.py:132
  283.1 8.2 %fusion.62 = f32[32,16,1,64]{3,2,1,0:T(1,128)S(1)} fusion(bf16[32,16,64,128]{3,2,1,0:T(8,128)(2,1)} %param.5, bf16[32,16,128,1]{2,1,0,3:T(8,128)(2,1)S(1)} %get-tuple-element.18), kind=kOutput, calls=%fused_computation.74 | convolution fusion | flops 8388608 | bytes 8650752 | tf_op jit(solution)/shard_map/pbkj,pkij->pbki/dot_general | solution.py:135
  294.8 3.9 copy.81
  298.7 2.7 reshape.426
  301.4 6.0 %all-to-all-start.1 = ((bf16[8,2,32768]{2,1,0:T(2,128)(2,1)}), bf16[8,2,32768]{2,1,0:T(2,128)(2,1)}, u32[]{:S(2)}, u32[]{:S(2)}) async-start(bf16[8,2,32768]{2,1,0:T(2,128)(2,1)} %reshape.426), calls=%async_computation.1 | async-start | bytes 2097152 | tf_op jit(solution)/shard_map/all_to_all | solution.py:140
  323.4 12.6 %add_convert_fusion = bf16[32,16,64,128]{3,2,1,0:T(8,128)(2,1)} fusion(f32[32,16,128]{2,1,0:T(8,128)} %get-tuple-element.19, f32[32,16,64]{2,1,0:T(8,128)S(1)} %copy.96, f32[32,16,128]{2,1,0:T(8,128)S(1)} %get-tuple-element.14, f32[32,16,64]{2,1,0:T(8,128)S(1)} %copy.95), kind=kLoop, calls=%fused_computation.5 | loop fusion | flops 16777216 | bytes 9175040 | tf_op jit(solution)/shard_map/convert_element_type | solution.py:129
  336.1 3.3 reshape.427
  340.3 4.4 fusion.51
  344.7 4.4 fusion.52
  349.2 5.2 %add_bitcast_fusion = f32[1,16,64,64,16]{3,2,4,1,0:T(8,128)S(1)} fusion(f32[16,64,16,64]{3,1,2,0:T(8,128)S(1)} %fusion.51, bf16[1,16,1,64,16,16]{3,5,4,2,1,0:T(8,128)(2,1)S(1)} %get-tuple-element.8, s32[16]{0:T(128)S(1)} %get-tuple-element.21), kind=kOutput, calls=%fused_computation.15 | convolution fusion | flops 202389504 | bytes 8912960 | tf_op jit(solution)/shard_map/kx,...ckm->...cxm/dot_general | solution.py:77
  354.4 4.9 subtract_bitcast_fusion
  359.3 3.3 maximum_bitcast_fusion
  362.6 58.2 %convert_bitcast_fusion = bf16[1,16,64,64,128]{4,3,2,1,0:T(8,128)(2,1)} fusion(f32[16,64,64,32]{2,1,3,0:T(8,128)S(1)} %maximum_bitcast_fusion, f32[16,128]{1,0:T(8,128)S(1)} %get-tuple-element.28, f32[16,128]{1,0:T(8,128)S(1)} %get-tuple-element.29), kind=kOutput, calls=%fused_computation.6 | convolution fusion | flops 3229622272 | bytes 25182208 | tf_op jit(solution)/shard_map/dot_general | solution.py:81
  420.8 69.6 %all-reduce.2.cloned.1.call-done = bf16[32,16,64,128]{3,2,1,0:T(8,128)(2,1)} async-done(((bf16[32,16,64,128]{3,2,1,0:T(8,128)(2,1)}), bf16[32,16,64,128]{3,2,1,0:T(8,128)(2,1)}) %all-reduce.2.cloned.1.call-update) | async-done | bytes 8388624 | tf_op jit(solution)/shard_map/psum | solution.py:128
  490.4 11.7 %convert_element_type.95 = f32[32,16,64,128]{3,2,1,0:T(8,128)} convert(bf16[32,16,64,128]{3,2,1,0:T(8,128)(2,1)} %all-reduce.2.cloned.1.call-done) | non-fusion elementwise | flops 4194304 | bytes 25165824 | tf_op jit(solution)/shard_map/convert_element_type | solution.py:130
  (53 shorter events, 34.9 us)
Async XLA Ops:
  34.5 42.0 %copy-start = (f32[16,64,64,32]{2,1,0,3:T(8,128)S(1)}, f32[16,64,64,32]{2,1,0,3:T(8,128)}, u32[]{:S(2)}) copy-start(f32[16,64,64,32]{2,1,0,3:T(8,128)} %reshape.397) | copy-start | bytes 25165828
  122.4 121.9 %all-to-all-start = ((bf16[8,2,32768]{2,1,0:T(2,128)(2,1)}), bf16[8,2,32768]{2,1,0:T(2,128)(2,1)S(1)}, u32[]{:S(2)}, u32[]{:S(2)}) async-start(bf16[8,2,32768]{2,1,0:T(2,128)(2,1)} %reshape.424), calls=%async_computation | async-start | bytes 2097152 | tf_op jit(solution)/shard_map/all_to_all | solution.py:122
  157.0 41.9 %copy-start.1 = (f32[16,64,64,32]{2,1,0,3:T(8,128)S(1)}, f32[16,64,64,32]{2,1,0,3:T(8,128)}, u32[]{:S(2)}) copy-start(f32[16,64,64,32]{2,1,0,3:T(8,128)} %reshape.406) | copy-start | bytes 25165828
  244.4 1.0 copy-start.2
  245.3 56.1 %all-to-all-start.2 = ((bf16[8,2,32768]{2,1,0:T(2,128)(2,1)}), bf16[8,2,32768]{2,1,0:T(2,128)(2,1)S(1)}, u32[]{:S(2)}, u32[]{:S(2)}) async-start(bf16[8,2,32768]{2,1,0:T(2,128)(2,1)} %reshape.428), calls=%async_computation.2 | async-start | bytes 2097152 | tf_op jit(solution)/shard_map/all_to_all | solution.py:121
  301.4 34.7 %all-to-all-start.1 = ((bf16[8,2,32768]{2,1,0:T(2,128)(2,1)}), bf16[8,2,32768]{2,1,0:T(2,128)(2,1)}, u32[]{:S(2)}, u32[]{:S(2)}) async-start(bf16[8,2,32768]{2,1,0:T(2,128)(2,1)} %reshape.426), calls=%async_computation.1 | async-start | bytes 2097152 | tf_op jit(solution)/shard_map/all_to_all | solution.py:140
  307.4 183.0 %all-reduce.2.cloned.1.call-start = ((), (), s32[]{:S(2)}) async-start(), calls=%async_computation.3 | async-start | bytes 16777216 | tf_op jit(solution)/shard_map/psum | solution.py:128
Sparse Core Ops, SparseCore 0:
  336.2 154.2 all-reduce.1
where the time goes:
time: 517 us; the launch traced here: 509 us
  matrix products  307 us (59%)
  waiting for transfers between devices  69.6 us (13%)
  local copies, waits for them, and re-layouts  66.4 us (13%)
  other arithmetic  32.5 us (6%)
  starting transfers between devices  19.3 us (4%)
  between operations  14.8 us (3%)
    dot_general x2, matrix products, plane_spectrum(): jnp.einsum('kx,...cxm->...ckm', sin_x, along_z, precision=highest)  83.9 us
    dot_general x2, matrix products, plane_spectrum(): jnp.einsum('kx,...cxm->...ckm', cos_x, along_z, precision=highest)  79.5 us
    psum x1, waiting for transfers between devices, local(): lax.psum(weight_terms(input_modes, cot_modes).astype(jnp.bfloat16), 'batch')  69.6 us
    dot_general x1, matrix products, plane_inverse(): jnp.dot(joined.reshape(-1, 2 * MZ), z_back, precision=highest, preferred_...  58.2 us
    dot_general x2, matrix products, plane_spectrum(): jnp.dot(values.reshape(-1, Z), z_table, preferred_element_type=jnp.float32)  30 us
    unnamed x16, local copies, waits for them, and re-layouts  27.2 us
    another operation x8, local copies, waits for them, and re-layouts  15.9 us
    convert_element_type x1, other arithmetic, local(): weight_terms(input_modes, cot_modes).astype(jnp.bfloat16)  12.6 us
  transfers between devices with their start and end apart: 4, of which 1 were waited for; matrix products, arithmetic and copies ran while one was open for 55% of the time, Pallas kernels for 0%

commit v1 on v0

--- a/solution.py
+++ b/solution.py
@@ -1,8 +1,12 @@
+import functools
 import math
 
 import jax
 import jax.numpy as jnp
+import numpy as np
 from jax import lax
+from jax.experimental import pallas as pl
+from jax.experimental.pallas import tpu as pltpu
 from jax.sharding import PartitionSpec as P
 
 C = 64
@@ -104,7 +108,7 @@
     return first_term + second_term
 
 
-def local(inputs, cotangent, mode_weights):
+def local_any(inputs, cotangent, mode_weights):
     inv_scale = 1.0 / math.sqrt(X * Y * Z)
     cos_z, sin_z = twiddles(jnp.arange(MZ), jnp.arange(Z), Z)
     z_table = jnp.concatenate([cos_z.T, -sin_z.T], axis=1).astype(jnp.bfloat16)
@@ -142,6 +146,470 @@
     return (input_grad, weight_grad)
 
 
+GROUP = 8
+ROWS = 16
+LANES = 128
+BLOCK = 4
+STEP = 4
+
+
+def angles_of(waves, length):
+    turns = 2.0 * np.pi / length * (np.outer(waves, np.arange(length)) % length)
+    return np.cos(turns), np.sin(turns)
+
+
+def signed_waves(retained, length):
+    return np.concatenate([np.arange(retained // 2), np.arange(length - retained // 2, length)])
+
+
+def as_table(array):
+    return np.asarray(array, np.float32).astype(jnp.bfloat16)
+
+
+def x_tables(length):
+    cos_x, sin_x = angles_of(signed_waves(MX, length), length)
+    unit = np.eye(GROUP)
+    both = np.stack([cos_x, sin_x])
+    forward = np.einsum("qkx,cd->qkcdx", both, unit).reshape(2 * MX * GROUP, GROUP * length)
+    both = np.stack([cos_x, -sin_x])
+    back = np.einsum("qkx,cd->dxqkc", both, unit).reshape(GROUP * length, 2 * MX * GROUP)
+    return as_table(forward), as_table(back)
+
+
+def z_tables(length, scale):
+    cos_z, sin_z = angles_of(np.arange(MZ), length)
+    forward = np.concatenate(
+        [np.concatenate([cos_z, -sin_z], axis=1), np.concatenate([-sin_z, -cos_z], axis=1)]
+    )
+    doubled = np.where(np.arange(MZ) == 0, 1.0, 2.0)[:, None]
+    doubled = np.concatenate([doubled, doubled])
+    back = np.concatenate(
+        [np.concatenate([cos_z, sin_z], axis=1), np.concatenate([-sin_z, cos_z], axis=1)]
+    )
+    return (
+        as_table(as_table(forward).astype(np.float32) * scale),
+        as_table(as_table(forward).astype(np.float32) * scale * doubled),
+        as_table(back * scale),
+    )
+
+
+def y_tables(length, shards):
+    cos_y, sin_y = angles_of(signed_waves(MY, length), length)
+    per = length // shards
+    real = np.stack([cos_y, sin_y], axis=1)
+    imag = np.stack([-sin_y, cos_y], axis=1)
+    rows = np.stack([real, imag], axis=1).reshape(2 * MY, 2, shards, per)
+    forward = rows.transpose(2, 0, 1, 3).reshape(shards, 2 * MY, 2 * per)
+    back = np.stack([np.stack([cos_y, -sin_y], axis=-1), np.stack([sin_y, cos_y], axis=-1)])
+    back = back.transpose(2, 0, 1, 3).reshape(shards, 2 * per, 2 * MY)
+    return as_table(forward), as_table(back)
+
+
+def peer_order(bits):
+    if not bits:
+        return [0]
+    kept = peer_order(bits[1:])
+    return kept + [distance ^ bits[0] for distance in kept]
+
+
+def gathered_order(bits):
+    held = [0]
+    for bit in bits:
+        held = held + [distance ^ bit for distance in held]
+    return held
+
+
+def dot(left, right, left_dim=1, right_dim=0):
+    dims = (((left_dim,), (right_dim,)), ((), ()))
+    return lax.dot_general(left, right, dims, preferred_element_type=jnp.float32)
+
+
+def spectrum_kernel(
+    planes, orders, me_ref, field_ref, x_ref, z_ref, y_ref, *refs
+):
+    step = pl.program_id(0)
+    block, channels, length, depth = field_ref.shape[1:]
+    *part_refs, rows_ref, total_ref = refs
+    shards, _, width = total_ref.shape
+    for plane in range(block):
+        for first in range(0, channels, 2 * GROUP):
+            sides = [
+                field_ref[0, plane, first + side * GROUP : first + (side + 1) * GROUP].reshape(
+                    GROUP * length, depth
+                )
+                for side in range(2)
+            ]
+            mixed = dot(x_ref[...], jnp.concatenate(sides, axis=1))
+            half = MX * GROUP
+            parts = [
+                jnp.concatenate(
+                    [
+                        mixed[:half, side * depth : (side + 1) * depth],
+                        mixed[half:, side * depth : (side + 1) * depth],
+                    ],
+                    axis=1,
+                ).reshape(MX, GROUP, 2 * depth)
+                for side in range(2)
+            ]
+            rows_ref[plane, :, first : first + 2 * GROUP, :] = jnp.concatenate(
+                parts, axis=1
+            ).astype(jnp.bfloat16)
+        modes = dot(z_ref[...], rows_ref[plane].reshape(MX * channels, 2 * depth), 1, 1)
+        for shard in range(shards):
+            total_ref[shard, pl.ds(step * block + plane, 2 * MZ, stride=planes), :] = modes[
+                :, shard * width : (shard + 1) * width
+            ]
+
+    @pl.when(step == pl.num_programs(0) - 1)
+    def _():
+        me = me_ref[0]
+        table = y_ref[me]
+        chunk = MZ // len(orders)
+        for stream, order in enumerate(orders):
+            for kz in range(chunk):
+                first = (stream * chunk + kz) * planes
+                parts = [
+                    jnp.concatenate(
+                        [
+                            total_ref[me ^ distance, pl.ds(part * MZ * planes + first, planes), :]
+                            for distance in order
+                        ],
+                        axis=1,
+                    )
+                    for part in range(2)
+                ]
+                modes = dot(table, jnp.concatenate(parts).astype(jnp.bfloat16))
+                modes = modes.astype(jnp.bfloat16)
+                for place in range(shards):
+                    side, place_in = divmod(place, shards // 2)
+                    part_refs[2 * stream + side][place_in, kz] = modes[
+                        :, place * width : (place + 1) * width
+                    ]
+
+
+def plane_modes(me, field, x_table, z_table, y_table, orders, block):
+    _, planes, channels, length, depth = field.shape
+    shards = len(orders[0])
+    width = MX * channels // shards
+    shape = (shards // 2, MZ // len(orders), 2 * MY, width)
+    whole = pl.BlockSpec(shape, lambda i: (0, 0, 0, 0))
+    return pl.pallas_call(
+        functools.partial(spectrum_kernel, planes, orders),
+        out_shape=[jax.ShapeDtypeStruct(shape, jnp.bfloat16)] * (2 * len(orders)),
+        grid=(planes // block,),
+        in_specs=[
+            pl.BlockSpec(memory_space=pltpu.SMEM),
+            pl.BlockSpec((1, block, channels, length, depth), lambda i: (0, i, 0, 0, 0)),
+            pl.BlockSpec(x_table.shape, lambda i: (0, 0)),
+            pl.BlockSpec(z_table.shape, lambda i: (0, 0)),
+            pl.BlockSpec(y_table.shape, lambda i: (0, 0, 0)),
+        ],
+        out_specs=[whole] * (2 * len(orders)),
+        scratch_shapes=[
+            pltpu.VMEM((block, MX, channels, 2 * depth), jnp.bfloat16),
+            pltpu.VMEM((shards, 2 * MZ * planes, width), jnp.float32),
+        ],
+        compiler_params=pltpu.CompilerParams(dimension_semantics=("arbitrary",)),
+        cost_estimate=pl.CostEstimate(
+            flops=2 * field.size * 8 * MX, bytes_accessed=2 * field.size, transcendentals=0
+        ),
+        name="plane_modes",
+    )(me, field, x_table, z_table, y_table)
+
+
+def swapped(array, bit, shards):
+    return lax.ppermute(array, "space", [(i, i ^ bit) for i in range(shards)])
+
+
+def total(keep, moved):
+    return (keep.astype(jnp.float32) + moved.astype(jnp.float32)).astype(jnp.bfloat16)
+
+
+def halved(keep, moved):
+    both = total(keep, moved)
+    half = both.shape[0] // 2
+    return both[:half], both[half:]
+
+
+def after(values):
+    return lax.optimization_barrier(values)
+
+
+def turned_rows(modes):
+    rows = modes.shape[0]
+    row = lax.broadcasted_iota(jnp.int32, modes.shape, 0)
+    return jnp.where(row % 2 == 0, pltpu.roll(modes, rows - 1, 0), -pltpu.roll(modes, 1, 0))
+
+
+def join_halves(plain, turned, side):
+    low = lax.broadcasted_iota(jnp.int32, plain.shape, 1) < LANES // 2
+    if side == 0:
+        return jnp.where(low, plain, pltpu.roll(turned, LANES // 2, 1))
+    return jnp.where(low, pltpu.roll(plain, LANES // 2, 1), turned)
+
+
+def mode_grad_kernel(keep_ref, moved_ref, w_ref, modes_ref, grad_ref):
+    _, chunk, _, channels, _ = w_ref.shape
+    row = lax.broadcasted_iota(jnp.int32, (2 * MY, MY * channels), 0) // 2
+    lane = lax.broadcasted_iota(jnp.int32, (2 * MY, MY * channels), 1) // channels
+    own = row == lane
+    low = lax.broadcasted_iota(jnp.int32, (2 * MY, LANES), 1) < LANES // 2
+    for kz in range(chunk):
+        plain = keep_ref[0, kz].astype(jnp.float32) + moved_ref[0, kz].astype(jnp.float32)
+        turned = turned_rows(plain)
+        modes_ref[kz] = plain.astype(jnp.bfloat16)
+        sides = []
+        for side in range(2):
+            left = join_halves(plain, turned, side).astype(jnp.bfloat16)
+            crossed = dot(left, w_ref[side, kz].reshape(MY * channels, 2 * channels), 1, 1)
+            crossed = jnp.where(own, crossed, 0.0)
+            kept = crossed[:, :LANES]
+            for first in range(LANES, MY * channels, LANES):
+                kept = kept + crossed[:, first : first + LANES]
+            sides.append(kept + pltpu.roll(kept, LANES // 2, 1))
+        grad_ref[0, kz] = jnp.where(low, sides[0], sides[1]).astype(jnp.bfloat16)
+
+
+def mode_grads(keep, moved, weights, first, chunk):
+    _, kinds, rows, width = keep.shape
+    channels = weights.shape[3]
+    part_spec = pl.BlockSpec((1, chunk, rows, width), lambda i: (0, i, 0, 0))
+    return pl.pallas_call(
+        mode_grad_kernel,
+        out_shape=(
+            jax.ShapeDtypeStruct(keep.shape[1:], jnp.bfloat16),
+            jax.ShapeDtypeStruct(keep.shape, jnp.bfloat16),
+        ),
+        grid=(kinds // chunk,),
+        in_specs=[
+            part_spec,
+            part_spec,
+            pl.BlockSpec(
+                (2, chunk, MY, channels, 2 * channels), lambda i: (0, i + first // chunk, 0, 0, 0)
+            ),
+        ],
+        out_specs=(pl.BlockSpec((chunk, rows, width), lambda i: (i, 0, 0)), part_spec),
+        compiler_params=pltpu.CompilerParams(dimension_semantics=("arbitrary",)),
+        cost_estimate=pl.CostEstimate(
+            flops=4 * MY * weights.size, bytes_accessed=weights.size, transcendentals=0
+        ),
+        name="mode_grads",
+    )(keep, moved, weights)
+
+
+def weight_kernel(channels, *refs):
+    *mode_refs, out_ref = refs
+    samples = len(mode_refs) // 2
+    for kz in range(out_ref.shape[1]):
+        inputs = jnp.concatenate([ref[kz] for ref in mode_refs[:samples]]).astype(jnp.float32)
+        cots = jnp.concatenate([ref[kz] for ref in mode_refs[samples:]]).astype(jnp.float32)
+        turned = turned_rows(cots)
+        wave = lax.broadcasted_iota(jnp.int32, cots.shape, 0) % (2 * MY) // 2
+        left = inputs.T.astype(jnp.bfloat16)
+        for side in range(2):
+            right = join_halves(cots, turned, side)
+            mine = left[side * channels : (side + 1) * channels]
+            for ky in range(0, MY, 2):
+                pair = [jnp.where(wave == ky + k, right, 0.0).astype(jnp.bfloat16) for k in range(2)]
+                grads = dot(mine, jnp.concatenate(pair, axis=1))
+                for k in range(2):
+                    out_ref[side, kz, ky + k] = grads[:, k * LANES : (k + 1) * LANES]
+
+
+def weight_grads(input_modes, cot_modes, channels, chunk):
+    samples = len(input_modes)
+    kinds, rows, width = input_modes[0].shape
+    shape = (2, kinds, MY, channels, 2 * channels)
+    return pl.pallas_call(
+        functools.partial(weight_kernel, channels),
+        out_shape=jax.ShapeDtypeStruct(shape, jnp.float32),
+        grid=(kinds // chunk,),
+        in_specs=[pl.BlockSpec((chunk, rows, width), lambda i: (i, 0, 0))] * (2 * samples),
+        out_specs=pl.BlockSpec((2, chunk, MY, channels, 2 * channels), lambda i: (0, i, 0, 0, 0)),
+        compiler_params=pltpu.CompilerParams(dimension_semantics=("arbitrary",)),
+        cost_estimate=pl.CostEstimate(
+            flops=2 * 128 * math.prod(shape), bytes_accessed=4 * math.prod(shape), transcendentals=0
+        ),
+        name="weight_grads",
+    )(*input_modes, *cot_modes)
+
+
+def inverse_kernel(orders, me_ref, *refs):
+    *held_refs, y_ref, z_ref, x_ref, out_ref, total_ref = refs
+    step = pl.program_id(0)
+    block, channels, length, depth = out_ref.shape[1:]
+    shards, _, width = total_ref.shape
+
+    @pl.when(step == 0)
+    def _():
+        me = me_ref[0]
+        table = y_ref[me]
+        chunk = MZ // len(orders)
+        for stream, order in enumerate(orders):
+            for kz in range(chunk):
+                modes = jnp.concatenate(
+                    [
+                        ref[place, kz]
+                        for ref in held_refs[2 * stream : 2 * stream + 2]
+                        for place in range(shards // 2)
+                    ],
+                    axis=1,
+                )
+                spread = dot(table, modes)
+                for place, distance in enumerate(order):
+                    rows = pl.ds(stream * chunk + kz, table.shape[0], stride=MZ)
+                    total_ref[me ^ distance, rows, :] = spread[
+                        :, place * width : (place + 1) * width
+                    ]
+
+    for plane in range(block):
+        rows = pl.ds((step * block + plane) * 2 * MZ, 2 * MZ)
+        modes = jnp.concatenate([total_ref[shard, rows, :] for shard in range(shards)], axis=1)
+        modes = modes.astype(jnp.bfloat16)
+        along = dot(modes, z_ref[...], 0, 0).reshape(MX, channels, 2 * depth)
+        for first in range(0, channels, 2 * GROUP):
+            sides = []
+            for side in range(2):
+                start = first + side * GROUP
+                piece = along[:, start : start + GROUP].reshape(MX * GROUP, 2 * depth)
+                sides.append(jnp.concatenate([piece[:, :depth], piece[:, depth:]], axis=0))
+            grads = dot(x_ref[...], jnp.concatenate(sides, axis=1).astype(jnp.bfloat16))
+            for side in range(2):
+                start = first + side * GROUP
+                out_ref[0, plane, start : start + GROUP] = (
+                    grads[:, side * depth : (side + 1) * depth]
+                    .reshape(GROUP, length, depth)
+                    .astype(jnp.bfloat16)
+                )
+
+
+def plane_grads(me, held, y_back, z_back, x_back, orders, shape, block):
+    _, planes, channels, length, depth = shape
+    shards = len(orders[0])
+    width = held[0].shape[-1]
+    return pl.pallas_call(
+        functools.partial(inverse_kernel, orders),
+        out_shape=jax.ShapeDtypeStruct(shape, jnp.bfloat16),
+        grid=(planes // block,),
+        in_specs=[pl.BlockSpec(memory_space=pltpu.SMEM)]
+        + [pl.BlockSpec(array.shape, lambda i: (0, 0, 0, 0)) for array in held]
+        + [
+            pl.BlockSpec(y_back.shape, lambda i: (0, 0, 0)),
+            pl.BlockSpec(z_back.shape, lambda i: (0, 0)),
+            pl.BlockSpec(x_back.shape, lambda i: (0, 0)),
+        ],
+        out_specs=pl.BlockSpec((1, block, channels, length, depth), lambda i: (0, i, 0, 0, 0)),
+        scratch_shapes=[pltpu.VMEM((shards, planes * 2 * MZ, width), jnp.float32)],
+        compiler_params=pltpu.CompilerParams(dimension_semantics=("arbitrary",)),
+        cost_estimate=pl.CostEstimate(
+            flops=2 * math.prod(shape) * 8 * MX,
+            bytes_accessed=2 * math.prod(shape),
+            transcendentals=0,
+        ),
+        name="plane_grads",
+    )(me, *held, y_back, z_back, x_back)
+
+
+def from_peers(array, groups):
+    others = [
+        lax.ppermute(array, "batch", [(i, i ^ k) for i in range(groups)]) for k in range(1, groups)
+    ]
+    return [array] + others
+
+
+def local_fast(shards, groups, inputs, cotangent, mode_weights):
+    _, planes, channels, length, depth = inputs.shape
+    scale = 1.0 / math.sqrt(length * planes * shards * depth)
+    x_table, x_back = x_tables(length)
+    z_plain, z_double, z_back = z_tables(depth, scale)
+    y_table, y_back = y_tables(planes * shards, shards)
+    me = lax.axis_index("space").reshape(1)
+    bits = [1 << place for place in range(shards.bit_length() - 1)]
+    paths = [bits, [bits[1], bits[0]] + bits[2:]]
+    down = [peer_order(path) for path in paths]
+    up = [gathered_order(path[::-1]) for path in paths]
+    streams = range(len(paths))
+
+    def split(parts):
+        return [parts[2 * k] for k in streams], [parts[2 * k + 1] for k in streams]
+
+    def reduce_step(keep, moved):
+        pairs = [halved(keep[k], moved[k]) for k in streams]
+        return [pair[0] for pair in pairs], [pair[1] for pair in pairs]
+
+    def swap_all(arrays, routes, step):
+        return [swapped(arrays[k], routes[k][step], shards) for k in streams]
+
+    keep, send = split(plane_modes(me, cotangent, x_table, z_double, y_table, down, BLOCK))
+    moved = swap_all(send, paths, 0)
+    parts = plane_modes(me, inputs, x_table, z_plain, y_table, down, BLOCK)
+    moved, parts = after((moved, parts))
+    input_keep, input_send = split(parts)
+    input_moved, input_sends = None, 0
+    for step in range(1, len(bits)):
+        keep, send = reduce_step(keep, moved)
+        if input_moved is None:
+            send, input_send = after((send, input_send))
+        else:
+            send, input_moved = after((send, input_moved))
+            input_keep, input_send = reduce_step(input_keep, input_moved)
+        moved = swap_all(send, paths, step)
+        input_moved = swap_all(input_send, paths, input_sends)
+        input_sends += 1
+    weights = mode_weights.reshape(2, MZ, MY, channels, 2 * channels)
+    chunk = MZ // len(paths)
+    cot_modes, held = [], []
+    for k in streams:
+        if k:
+            keep[k], cot_modes[-1] = after((keep[k], cot_modes[-1]))
+        else:
+            keep[k], input_send = after((keep[k], input_send))
+        modes, grad = mode_grads(keep[k], moved[k], weights, k * chunk, STEP)
+        cot_modes.append(modes)
+        held.append(grad)
+    routes = [path[::-1] for path in paths]
+    came = swap_all(held, routes, 0)
+    while input_sends < len(bits):
+        input_moved, cot_modes[-1] = after((input_moved, cot_modes[-1]))
+        input_keep, input_send = reduce_step(input_keep, input_moved)
+        input_moved = swap_all(input_send, paths, input_sends)
+        input_sends += 1
+    all_cots = from_peers(jnp.concatenate(cot_modes), groups)
+    input_modes = None
+    for step in range(1, len(bits)):
+        held = [jnp.concatenate([held[k], came[k]]) for k in streams]
+        came = swap_all(held, routes, step)
+        if step == 1:
+            input_moved, held = after((input_moved, held))
+            input_modes = jnp.concatenate([total(input_keep[k][0], input_moved[k][0]) for k in streams])
+            all_inputs = from_peers(input_modes, groups)
+    all_inputs, held = after((all_inputs, held))
+    weight_grad = weight_grads(all_inputs, all_cots, channels, STEP)
+    came, weight_grad = after((came, weight_grad))
+    gathered = [array for k in streams for array in (held[k], came[k])]
+    input_grad = plane_grads(
+        me, gathered, y_back, z_back, x_back, up, inputs.shape, BLOCK
+    )
+    return (input_grad, weight_grad.reshape(mode_weights.shape))
+
+
+def local(shards, groups, inputs, cotangent, mode_weights):
+    samples, planes, channels, _, depth = inputs.shape
+    fits = (
+        samples == 1
+        and planes % ROWS == 0
+        and MX % shards == 0
+        and MX // shards * channels == LANES
+        and depth == LANES
+        and shards > 2
+        and shards & (shards - 1) == 0
+        and groups & (groups - 1) == 0
+    )
+    if fits:
+        return local_fast(shards, groups, inputs, cotangent, mode_weights)
+    return local_any(inputs, cotangent, mode_weights)
+
+
 def solution(mesh):
     placed = (
         P("batch", "space", None, None, None),
@@ -149,7 +617,7 @@
         P("space", None, None, None),
     )
     return jax.shard_map(
-        local,
+        functools.partial(local, mesh.shape["space"], mesh.shape["batch"]),
         mesh=mesh,
         in_specs=placed,
         out_specs=(P("batch", "space", None, None, None), P("space", None, None, None)),

time: 517 us -> 118 us (0.23); the launches traced: 509 us -> 118 us
  matrix products: 307 us -> 0 us
  Pallas kernels: 0 us -> 58.1 us
  local copies, waits for them, and re-layouts: 66.4 us -> 8.81 us
  waiting for transfers between devices: 69.6 us -> 21.4 us
  other arithmetic: 32.5 us -> 2.4 us
  between operations: 14.8 us -> 0.97 us
  starting transfers between devices: 19.3 us -> 25.9 us
    dot_general x25 -> x0, matrix products: 307 us -> none  [the longest x2 83.9 us: plane_spectrum(): jnp.einsum('kx,...cxm->...ckm', sin_x, along_z, precision=highest)]
    psum x1 -> x0, waiting for transfers between devices: 69.6 us -> none  [local(): lax.psum(weight_terms(input_modes, cot_modes).astype(jnp.bfloat16), 'batch')]
    pallas_call x0 -> x6, Pallas kernels: none -> 58.1 us  [the longest x2 26.5 us: plane_modes(): pl.pallas_call(functools.partial(spectrum_kernel, planes, orders), out_sh...]
    ppermute x0 -> x24, starting transfers between devices: none -> 25.9 us  [the longest x18 23.6 us: swapped(): return lax.ppermute(array, 'space', [(i, i ^ bit) for i in range(shards)])]
    another operation x11 -> x0, local copies, waits for them, and re-layouts: 22.5 us -> none
    convert_element_type x2 -> x9, other arithmetic: 24.4 us -> 2.39 us  [total(): (keep.astype(jnp.float32) + moved.astype(jnp.float32)).astype(jnp.bfloat16)]
    ppermute x0 -> x24, waiting for transfers between devices: none -> 21.4 us  [the longest x18 12 us: swapped(): return lax.ppermute(array, 'space', [(i, i ^ bit) for i in range(shards)])]
    unnamed x16 -> x37, local copies, waits for them, and re-layouts: 27.2 us -> 6.56 us
  transfers between devices with their start and end apart: 4 -> 24, of which waited for: 1 -> 12; matrix products, arithmetic and copies ran while one was open for 55% -> 6% of each run, Pallas kernels for 0% -> 25%
where the time goes in v1:
time: 118 us
  Pallas kernels  58.1 us (49%)
  starting transfers between devices  25.9 us (22%)
  waiting for transfers between devices  21.4 us (18%)
  local copies, waits for them, and re-layouts  8.81 us (7%)
  other arithmetic  2.4 us (2%)
    pallas_call x2, Pallas kernels, plane_modes(): pl.pallas_call(functools.partial(spectrum_kernel, planes, orders), out_sh...  26.5 us
    ppermute x18, starting transfers between devices, swapped(): return lax.ppermute(array, 'space', [(i, i ^ bit) for i in range(shards)])  23.6 us
    pallas_call x1, Pallas kernels, plane_grads(): pl.pallas_call(functools.partial(inverse_kernel, orders), out_shape=jax.S...  15.4 us
    ppermute x18, waiting for transfers between devices, swapped(): return lax.ppermute(array, 'space', [(i, i ^ bit) for i in range(shards)])  12 us
    ppermute x6, waiting for transfers between devices, from_peers(): lax.ppermute(array, 'batch', [(i, i ^ k) for i in range(groups)])  9.46 us
    pallas_call x2, Pallas kernels, mode_grads(): pl.pallas_call(mode_grad_kernel, out_shape=(jax.ShapeDtypeStruct(keep.sha...  8.27 us
    pallas_call x1, Pallas kernels, weight_grads(): pl.pallas_call(functools.partial(weight_kernel, channels), out_shape=jax....  7.88 us
    unnamed x37, local copies, waits for them, and re-layouts  6.56 us
  transfers between devices with their start and end apart: 24, of which 12 were waited for; matrix products, arithmetic and copies ran while one was open for 6% of the time, Pallas kernels for 25%

profile of v1, /device:TPU:0, one launch (start us, length us, event | category | flops | bytes accessed | tf_op | source)
XLA Modules:
  0.0 117.6 jit_solution(17135898471855628438)
XLA Ops:
  0.6 13.3 %plane_modes.2 = (bf16[4,8,32,128]{3,2,1,0:T(8,128)(2,1)}, bf16[4,8,32,128]{3,2,1,0:T(8,128)(2,1)}, bf16[4,8,32,128]{3,2,1,0:T(8,128)(2,1)}, bf16[4,8,32,128]{3,2,1,0:T(8,128)(2,1)}) custom-call(s32[1]{0:T(128)} %bitcast.me_ref, bf16[1,16,64,64,128]{4,3,2,1,0:T(8,128)(2,1)} %field_ref.2, bf16[256,512]{1,0:T(8,128)(2,1)} %constant.18.clone.x_ref, ...), custom_call_target="tpu_custom_call" | custom-call | flops 2147483648 | bytes 16777216 | tf_op jit(solution)/shard_map/plane_modes/pallas_call | solution.py:296
  13.9 3.0 %collective-permute-start = (bf16[4,8,32,128]{3,2,1,0:T(8,128)(2,1)}, bf16[4,8,32,128]{3,2,1,0:T(8,128)(2,1)S(1)}, u32[]{:S(2)}, u32[]{:S(2)}) collective-permute-start(bf16[4,8,32,128]{3,2,1,0:T(8,128)(2,1)} %get-tuple-element.47), channel_id=1, source_target_pairs={{0,1},{1,0},{2,3},{3,2},{4,5},{5,4},{6,7},{7,6},{8,9},{9,8},{10,11... | collective-permute-start | bytes 786440 | tf_op jit(solution)/shard_map/ppermute | solution.py:321
  16.9 1.6 %collective-permute-start.1 = (bf16[4,8,32,128]{3,2,1,0:T(8,128)(2,1)}, bf16[4,8,32,128]{3,2,1,0:T(8,128)(2,1)S(1)}, u32[]{:S(2)}, u32[]{:S(2)}) collective-permute-start(bf16[4,8,32,128]{3,2,1,0:T(8,128)(2,1)} %get-tuple-element.48), channel_id=1, source_target_pairs={{0,2},{1,3},{2,0},{3,1},{4,6},{5,7},{6,4},{7,5},{8,10},{9,11},{10,... | collective-permute-start | bytes 786440 | tf_op jit(solution)/shard_map/ppermute | solution.py:321
  18.5 13.3 %plane_modes.3 = (bf16[4,8,32,128]{3,2,1,0:T(8,128)(2,1)}, bf16[4,8,32,128]{3,2,1,0:T(8,128)(2,1)}, bf16[4,8,32,128]{3,2,1,0:T(8,128)(2,1)}, bf16[4,8,32,128]{3,2,1,0:T(8,128)(2,1)}) custom-call(s32[1]{0:T(128)} %bitcast.me_ref, bf16[1,16,64,64,128]{4,3,2,1,0:T(8,128)(2,1)} %field_ref.3, bf16[256,512]{1,0:T(8,128)(2,1)} %constant.18.clone.x_ref, ...), custom_call_target="tpu_custom_call" | custom-call | flops 2147483648 | bytes 16777216 | tf_op jit(solution)/shard_map/plane_modes/pallas_call | solution.py:296
  32.6 1.9 %collective-permute-start.4 = (bf16[4,8,32,128]{3,2,1,0:T(8,128)(2,1)}, bf16[4,8,32,128]{3,2,1,0:T(8,128)(2,1)S(1)}, u32[]{:S(2)}, u32[]{:S(2)}) collective-permute-start(bf16[4,8,32,128]{3,2,1,0:T(8,128)(2,1)} %get-tuple-element.62), channel_id=1, source_target_pairs={{0,1},{1,0},{2,3},{3,2},{4,5},{5,4},{6,7},{7,6},{8,9},{9,8},{10,11... | collective-permute-start | bytes 786440 | tf_op jit(solution)/shard_map/ppermute | solution.py:321
  34.5 1.6 %collective-permute-start.5 = (bf16[4,8,32,128]{3,2,1,0:T(8,128)(2,1)}, bf16[4,8,32,128]{3,2,1,0:T(8,128)(2,1)S(1)}, u32[]{:S(2)}, u32[]{:S(2)}) collective-permute-start(bf16[4,8,32,128]{3,2,1,0:T(8,128)(2,1)} %get-tuple-element.63), channel_id=1, source_target_pairs={{0,2},{1,3},{2,0},{3,1},{4,6},{5,7},{6,4},{7,5},{8,10},{9,11},{10,... | collective-permute-start | bytes 786440 | tf_op jit(solution)/shard_map/ppermute | solution.py:321
  36.1 2.2 %collective-permute-done.2 = bf16[2,8,32,128]{3,2,1,0:T(8,128)(2,1)S(1)} collective-permute-done((bf16[2,8,32,128]{3,2,1,0:T(8,128)(2,1)S(1)}, bf16[2,8,32,128]{3,2,1,0:T(8,128)(2,1)S(1)}, u32[]{:S(2)}, u32[]{:S(2)}) %collective-permute-start.2) | collective-permute-done | bytes 131104 | tf_op jit(solution)/shard_map/ppermute | solution.py:321
  40.2 2.3 %collective-permute-done.4 = bf16[4,8,32,128]{3,2,1,0:T(8,128)(2,1)S(1)} collective-permute-done((bf16[4,8,32,128]{3,2,1,0:T(8,128)(2,1)}, bf16[4,8,32,128]{3,2,1,0:T(8,128)(2,1)S(1)}, u32[]{:S(2)}, u32[]{:S(2)}) %collective-permute-start.4) | collective-permute-done | bytes 262176 | tf_op jit(solution)/shard_map/ppermute | solution.py:321
  42.6 2.6 %collective-permute-start.8 = (bf16[1,8,32,128]{3,2,1,0:T(8,128)(2,1)S(1)}, bf16[1,8,32,128]{3,2,1,0:T(8,128)(2,1)S(1)}, u32[]{:S(2)}, u32[]{:S(2)}) collective-permute-start(bf16[1,8,32,128]{3,2,1,0:T(8,128)(2,1)S(1)} %get-tuple-element.68), channel_id=1, source_target_pairs={{0,4},{1,5},{2,6},{3,7},{4,0},{5,1},{6,2},{7,3},{8,12},{9,13},{10,... | collective-permute-start | bytes 196616 | tf_op jit(solution)/shard_map/ppermute | solution.py:321
  45.6 1.0 add_convert_fusion.1
  46.6 1.0 add_convert_fusion
  47.6 1.5 %collective-permute-start.6 = (bf16[2,8,32,128]{3,2,1,0:T(8,128)(2,1)S(1)}, bf16[2,8,32,128]{3,2,1,0:T(8,128)(2,1)S(1)}, u32[]{:S(2)}, u32[]{:S(2)}) collective-permute-start(bf16[2,8,32,128]{3,2,1,0:T(8,128)(2,1)S(1)} %slice.71), channel_id=1, source_target_pairs={{0,2},{1,3},{2,0},{3,1},{4,6},{5,7},{6,4},{7,5},{8,10},{9,11},{10,... | collective-permute-start | bytes 393224 | tf_op jit(solution)/shard_map/ppermute | solution.py:321
  50.4 4.1 %mode_grads.2 = (bf16[8,32,128]{2,1,0:T(8,128)(2,1)}, bf16[1,8,32,128]{3,2,1,0:T(8,128)(2,1)}) custom-call(bf16[1,8,32,128]{3,2,1,0:T(8,128)(2,1)} %get-tuple-element.67.keep_ref, bf16[1,8,32,128]{3,2,1,0:T(8,128)(2,1)} %copy-done.15, bf16[2,16,16,64,128]{4,3,2,1,0:T(8,128)(2,1)} %bitcast.7), custom_call_target="tpu_custom_call" | custom-call | flops 268435456 | bytes 4194304 | tf_op jit(solution)/shard_map/mode_grads/pallas_call | solution.py:377
  55.2 4.1 %mode_grads.3 = (bf16[8,32,128]{2,1,0:T(8,128)(2,1)}, bf16[1,8,32,128]{3,2,1,0:T(8,128)(2,1)}) custom-call(bf16[1,8,32,128]{3,2,1,0:T(8,128)(2,1)} %get-tuple-element.70.keep_ref, bf16[1,8,32,128]{3,2,1,0:T(8,128)(2,1)} %copy-done.14, bf16[2,16,16,64,128]{4,3,2,1,0:T(8,128)(2,1)} %bitcast.8), custom_call_target="tpu_custom_call" | custom-call | flops 268435456 | bytes 4194304 | tf_op jit(solution)/shard_map/mode_grads/pallas_call | solution.py:377
  59.3 2.5 %collective-permute-start.13 = (bf16[1,8,32,128]{3,2,1,0:T(8,128)(2,1)}, bf16[1,8,32,128]{3,2,1,0:T(8,128)(2,1)S(1)}, u32[]{:S(2)}, u32[]{:S(2)}) collective-permute-start(bf16[1,8,32,128]{3,2,1,0:T(8,128)(2,1)} %get-tuple-element.76), channel_id=1, source_target_pairs={{0,4},{1,5},{2,6},{3,7},{4,0},{5,1},{6,2},{7,3},{8,12},{9,13},{10,... | collective-permute-start | bytes 196616 | tf_op jit(solution)/shard_map/ppermute | solution.py:321
  61.9 0.9 constant_dynamic-update-slice_fusion.3
  63.1 0.9 constant_dynamic-update-slice_fusion.1
  64.0 0.8 constant_dynamic-update-slice_fusion.9
  64.9 3.8 %collective-permute-done.12 = bf16[1,8,32,128]{3,2,1,0:T(8,128)(2,1)S(1)} collective-permute-done((bf16[1,8,32,128]{3,2,1,0:T(8,128)(2,1)}, bf16[1,8,32,128]{3,2,1,0:T(8,128)(2,1)S(1)}, u32[]{:S(2)}, u32[]{:S(2)}) %collective-permute-start.12) | collective-permute-done | bytes 65568 | tf_op jit(solution)/shard_map/ppermute | solution.py:321
  68.7 0.9 collective-permute-start.17
  70.4 2.3 %collective-permute-start.10 = (bf16[1,8,32,128]{3,2,1,0:T(8,128)(2,1)S(1)}, bf16[1,8,32,128]{3,2,1,0:T(8,128)(2,1)S(1)}, u32[]{:S(2)}, u32[]{:S(2)}) collective-permute-start(bf16[1,8,32,128]{3,2,1,0:T(8,128)(2,1)S(1)} %slice.76), channel_id=1, source_target_pairs={{0,4},{1,5},{2,6},{3,7},{4,0},{5,1},{6,2},{7,3},{8,12},{9,13},{10,... | collective-permute-start | bytes 196616 | tf_op jit(solution)/shard_map/ppermute | solution.py:321
  72.7 1.5 %collective-permute-start.18 = (bf16[2,8,32,128]{3,2,1,0:T(8,128)(2,1)S(1)}, bf16[2,8,32,128]{3,2,1,0:T(8,128)(2,1)S(1)}, u32[]{:S(2)}, u32[]{:S(2)}) collective-permute-start(bf16[2,8,32,128]{3,2,1,0:T(8,128)(2,1)S(1)} %constant_dynamic-update-slice_fusion.2), channel_id=1, source_target_pairs={{0,1},{1,0},{2,3},{3,2},{4,5},{5,4},{6,7},{7,6},{8,9},{9,8},{10,11... | collective-permute-start | bytes 393224 | tf_op jit(solution)/shard_map/ppermute | solution.py:321
  74.9 2.1 %collective-permute-done.10 = bf16[1,8,32,128]{3,2,1,0:T(8,128)(2,1)S(1)} collective-permute-done((bf16[1,8,32,128]{3,2,1,0:T(8,128)(2,1)S(1)}, bf16[1,8,32,128]{3,2,1,0:T(8,128)(2,1)S(1)}, u32[]{:S(2)}, u32[]{:S(2)}) %collective-permute-start.10) | collective-permute-done | bytes 65568 | tf_op jit(solution)/shard_map/ppermute | solution.py:321
  77.2 1.5 %collective-permute-start.15 = (bf16[16,32,128]{2,1,0:T(8,128)(2,1)S(1)}, bf16[16,32,128]{2,1,0:T(8,128)(2,1)S(1)}, u32[]{:S(2)}, u32[]{:S(2)}) collective-permute-start(bf16[16,32,128]{2,1,0:T(8,128)(2,1)S(1)} %pad_maximum_fusion.refs_0_), channel_id=1, source_target_pairs={{0,16},{8,24},{16,0},{24,8},{1,17},{9,25},{17,1},{25,9},{2,18},{10... | collective-permute-start | bytes 393224 | tf_op jit(solution)/shard_map/ppermute | solution.py:515
  79.2 1.6 %collective-permute-start.19 = (bf16[4,8,32,128]{3,2,1,0:T(8,128)(2,1)S(1)}, bf16[4,8,32,128]{3,2,1,0:T(8,128)(2,1)S(1)}, u32[]{:S(2)}, u32[]{:S(2)}) collective-permute-start(bf16[4,8,32,128]{3,2,1,0:T(8,128)(2,1)S(1)} %constant_dynamic-update-slice_fusion.4.refs_0_), channel_id=1, source_target_pairs={{0,1},{1,0},{2,3},{3,2},{4,5},{5,4},{6,7},{7,6},{8,9},{9,8},{10,11... | collective-permute-start | bytes 786440 | tf_op jit(solution)/shard_map/ppermute | solution.py:321
  80.8 0.9 constant_dynamic-update-slice_fusion.8.refs_4_
  81.7 1.3 %collective-permute-done.16.refs_3_ = bf16[16,32,128]{2,1,0:T(8,128)(2,1)S(1)} collective-permute-done((bf16[16,32,128]{2,1,0:T(8,128)(2,1)S(1)}, bf16[16,32,128]{2,1,0:T(8,128)(2,1)S(1)}, u32[]{:S(2)}, u32[]{:S(2)}) %collective-permute-start.16) | collective-permute-done | bytes 131104 | tf_op jit(solution)/shard_map/ppermute | solution.py:515
  82.9 2.8 %collective-permute-done.15.refs_2_ = bf16[16,32,128]{2,1,0:T(8,128)(2,1)S(1)} collective-permute-done((bf16[16,32,128]{2,1,0:T(8,128)(2,1)S(1)}, bf16[16,32,128]{2,1,0:T(8,128)(2,1)S(1)}, u32[]{:S(2)}, u32[]{:S(2)}) %collective-permute-start.15) | collective-permute-done | bytes 131104 | tf_op jit(solution)/shard_map/ppermute | solution.py:515
  86.2 2.2 %collective-permute-done.23.refs_7_ = bf16[16,32,128]{2,1,0:T(8,128)(2,1)S(1)} collective-permute-done((bf16[16,32,128]{2,1,0:T(8,128)(2,1)S(1)}, bf16[16,32,128]{2,1,0:T(8,128)(2,1)S(1)}, u32[]{:S(2)}, u32[]{:S(2)}) %collective-permute-start.23) | collective-permute-done | bytes 131104 | tf_op jit(solution)/shard_map/ppermute | solution.py:515
  88.4 3.2 %collective-permute-done.22.refs_6_ = bf16[16,32,128]{2,1,0:T(8,128)(2,1)S(1)} collective-permute-done((bf16[16,32,128]{2,1,0:T(8,128)(2,1)S(1)}, bf16[16,32,128]{2,1,0:T(8,128)(2,1)S(1)}, u32[]{:S(2)}, u32[]{:S(2)}) %collective-permute-start.22) | collective-permute-done | bytes 131104 | tf_op jit(solution)/shard_map/ppermute | solution.py:515
  92.9 7.9 %weight_grads.1 = f32[2,16,16,64,128]{4,3,2,1,0:T(8,128)} custom-call(bf16[16,32,128]{2,1,0:T(8,128)(2,1)} %copy-done.2, bf16[16,32,128]{2,1,0:T(8,128)(2,1)} %copy-done.10, bf16[16,32,128]{2,1,0:T(8,128)(2,1)} %copy-done.9, bf16[16,32,128]{2,1,0:T(8,128)(2,1)} %copy-done.8, bf16[16,32,128]{2,1,0:T(8,128)(2,1)} %copy-done.3, ...), custom_call_target="tpu_custom_call" | custom-call | flops 1073741824 | bytes 16777216 | tf_op jit(solution)/shard_map/weight_grads/pallas_call | solution.py:423
  102.2 15.4 %plane_grads.1 = bf16[1,16,64,64,128]{4,3,2,1,0:T(8,128)(2,1)} custom-call(s32[1]{0:T(128)} %bitcast.me_ref, bf16[4,8,32,128]{3,2,1,0:T(8,128)(2,1)} %copy-done, bf16[4,8,32,128]{3,2,1,0:T(8,128)(2,1)} %copy-done.5, bf16[4,8,32,128]{3,2,1,0:T(8,128)(2,1)} %copy-done.1, bf16[4,8,32,128]{3,2,1,0:T(8,128)(2,1)} %copy-done.4, ...), custom_call_target="tpu_custom_call" | custom-call | flops 2147483648 | bytes 16777216 | tf_op jit(solution)/shard_map/plane_grads/pallas_call | solution.py:490
  (82 shorter events, 10.8 us)
Async XLA Ops:
  13.9 17.9 %copy-start.6 = (bf16[4,8,32,128]{3,2,1,0:T(8,128)(2,1)S(1)}, bf16[4,8,32,128]{3,2,1,0:T(8,128)(2,1)}, u32[]{:S(2)}) copy-start(bf16[4,8,32,128]{3,2,1,0:T(8,128)(2,1)} %get-tuple-element.54) | copy-start | bytes 786436
  13.9 17.9 %copy-start.7 = (bf16[4,8,32,128]{3,2,1,0:T(8,128)(2,1)S(1)}, bf16[4,8,32,128]{3,2,1,0:T(8,128)(2,1)}, u32[]{:S(2)}) copy-start(bf16[4,8,32,128]{3,2,1,0:T(8,128)(2,1)} %get-tuple-element.56) | copy-start | bytes 786436
  13.9 17.9 %collective-permute-start = (bf16[4,8,32,128]{3,2,1,0:T(8,128)(2,1)}, bf16[4,8,32,128]{3,2,1,0:T(8,128)(2,1)S(1)}, u32[]{:S(2)}, u32[]{:S(2)}) collective-permute-start(bf16[4,8,32,128]{3,2,1,0:T(8,128)(2,1)} %get-tuple-element.47), channel_id=1, source_target_pairs={{0,1},{1,0},{2,3},{3,2},{4,5},{5,4},{6,7},{7,6},{8,9},{9,8},{10,11... | collective-permute-start | bytes 786440 | tf_op jit(solution)/shard_map/ppermute | solution.py:321
  16.9 14.8 %collective-permute-start.1 = (bf16[4,8,32,128]{3,2,1,0:T(8,128)(2,1)}, bf16[4,8,32,128]{3,2,1,0:T(8,128)(2,1)S(1)}, u32[]{:S(2)}, u32[]{:S(2)}) collective-permute-start(bf16[4,8,32,128]{3,2,1,0:T(8,128)(2,1)} %get-tuple-element.48), channel_id=1, source_target_pairs={{0,2},{1,3},{2,0},{3,1},{4,6},{5,7},{6,4},{7,5},{8,10},{9,11},{10,... | collective-permute-start | bytes 786440 | tf_op jit(solution)/shard_map/ppermute | solution.py:321
  32.0 6.3 %collective-permute-start.2 = (bf16[2,8,32,128]{3,2,1,0:T(8,128)(2,1)S(1)}, bf16[2,8,32,128]{3,2,1,0:T(8,128)(2,1)S(1)}, u32[]{:S(2)}, u32[]{:S(2)}) collective-permute-start(bf16[2,8,32,128]{3,2,1,0:T(8,128)(2,1)S(1)} %slice.65), channel_id=1, source_target_pairs={{0,2},{1,3},{2,0},{3,1},{4,6},{5,7},{6,4},{7,5},{8,10},{9,11},{10,... | collective-permute-start | bytes 393224 | tf_op jit(solution)/shard_map/ppermute | solution.py:321
  32.5 6.4 %collective-permute-start.3 = (bf16[2,8,32,128]{3,2,1,0:T(8,128)(2,1)S(1)}, bf16[2,8,32,128]{3,2,1,0:T(8,128)(2,1)S(1)}, u32[]{:S(2)}, u32[]{:S(2)}) collective-permute-start(bf16[2,8,32,128]{3,2,1,0:T(8,128)(2,1)S(1)} %slice.66), channel_id=1, source_target_pairs={{0,1},{1,0},{2,3},{3,2},{4,5},{5,4},{6,7},{7,6},{8,9},{9,8},{10,11... | collective-permute-start | bytes 393224 | tf_op jit(solution)/shard_map/ppermute | solution.py:321
  32.6 9.9 %collective-permute-start.4 = (bf16[4,8,32,128]{3,2,1,0:T(8,128)(2,1)}, bf16[4,8,32,128]{3,2,1,0:T(8,128)(2,1)S(1)}, u32[]{:S(2)}, u32[]{:S(2)}) collective-permute-start(bf16[4,8,32,128]{3,2,1,0:T(8,128)(2,1)} %get-tuple-element.62), channel_id=1, source_target_pairs={{0,1},{1,0},{2,3},{3,2},{4,5},{5,4},{6,7},{7,6},{8,9},{9,8},{10,11... | collective-permute-start | bytes 786440 | tf_op jit(solution)/shard_map/ppermute | solution.py:321
  34.5 8.1 %collective-permute-start.5 = (bf16[4,8,32,128]{3,2,1,0:T(8,128)(2,1)}, bf16[4,8,32,128]{3,2,1,0:T(8,128)(2,1)S(1)}, u32[]{:S(2)}, u32[]{:S(2)}) collective-permute-start(bf16[4,8,32,128]{3,2,1,0:T(8,128)(2,1)} %get-tuple-element.63), channel_id=1, source_target_pairs={{0,2},{1,3},{2,0},{3,1},{4,6},{5,7},{6,4},{7,5},{8,10},{9,11},{10,... | collective-permute-start | bytes 786440 | tf_op jit(solution)/shard_map/ppermute | solution.py:321
  42.6 7.2 %collective-permute-start.8 = (bf16[1,8,32,128]{3,2,1,0:T(8,128)(2,1)S(1)}, bf16[1,8,32,128]{3,2,1,0:T(8,128)(2,1)S(1)}, u32[]{:S(2)}, u32[]{:S(2)}) collective-permute-start(bf16[1,8,32,128]{3,2,1,0:T(8,128)(2,1)S(1)} %get-tuple-element.68), channel_id=1, source_target_pairs={{0,4},{1,5},{2,6},{3,7},{4,0},{5,1},{6,2},{7,3},{8,12},{9,13},{10,... | collective-permute-start | bytes 196616 | tf_op jit(solution)/shard_map/ppermute | solution.py:321
  45.2 9.3 %collective-permute-start.9 = (bf16[1,8,32,128]{3,2,1,0:T(8,128)(2,1)S(1)}, bf16[1,8,32,128]{3,2,1,0:T(8,128)(2,1)S(1)}, u32[]{:S(2)}, u32[]{:S(2)}) collective-permute-start(bf16[1,8,32,128]{3,2,1,0:T(8,128)(2,1)S(1)} %get-tuple-element.71), channel_id=1, source_target_pairs={{0,4},{1,5},{2,6},{3,7},{4,0},{5,1},{6,2},{7,3},{8,12},{9,13},{10,... | collective-permute-start | bytes 196616 | tf_op jit(solution)/shard_map/ppermute | solution.py:321
  47.6 21.9 %collective-permute-start.6 = (bf16[2,8,32,128]{3,2,1,0:T(8,128)(2,1)S(1)}, bf16[2,8,32,128]{3,2,1,0:T(8,128)(2,1)S(1)}, u32[]{:S(2)}, u32[]{:S(2)}) collective-permute-start(bf16[2,8,32,128]{3,2,1,0:T(8,128)(2,1)S(1)} %slice.71), channel_id=1, source_target_pairs={{0,2},{1,3},{2,0},{3,1},{4,6},{5,7},{6,4},{7,5},{8,10},{9,11},{10,... | collective-permute-start | bytes 393224 | tf_op jit(solution)/shard_map/ppermute | solution.py:321
  49.2 20.4 %collective-permute-start.7 = (bf16[2,8,32,128]{3,2,1,0:T(8,128)(2,1)S(1)}, bf16[2,8,32,128]{3,2,1,0:T(8,128)(2,1)S(1)}, u32[]{:S(2)}, u32[]{:S(2)}) collective-permute-start(bf16[2,8,32,128]{3,2,1,0:T(8,128)(2,1)S(1)} %slice.72), channel_id=1, source_target_pairs={{0,1},{1,0},{2,3},{3,2},{4,5},{5,4},{6,7},{7,6},{8,9},{9,8},{10,11... | collective-permute-start | bytes 393224 | tf_op jit(solution)/shard_map/ppermute | solution.py:321
  59.3 13.3 %collective-permute-start.13 = (bf16[1,8,32,128]{3,2,1,0:T(8,128)(2,1)}, bf16[1,8,32,128]{3,2,1,0:T(8,128)(2,1)S(1)}, u32[]{:S(2)}, u32[]{:S(2)}) collective-permute-start(bf16[1,8,32,128]{3,2,1,0:T(8,128)(2,1)} %get-tuple-element.76), channel_id=1, source_target_pairs={{0,4},{1,5},{2,6},{3,7},{4,0},{5,1},{6,2},{7,3},{8,12},{9,13},{10,... | collective-permute-start | bytes 196616 | tf_op jit(solution)/shard_map/ppermute | solution.py:321
  62.7 5.9 %collective-permute-start.12 = (bf16[1,8,32,128]{3,2,1,0:T(8,128)(2,1)}, bf16[1,8,32,128]{3,2,1,0:T(8,128)(2,1)S(1)}, u32[]{:S(2)}, u32[]{:S(2)}) collective-permute-start(bf16[1,8,32,128]{3,2,1,0:T(8,128)(2,1)} %get-tuple-element.75), channel_id=1, source_target_pairs={{0,4},{1,5},{2,6},{3,7},{4,0},{5,1},{6,2},{7,3},{8,12},{9,13},{10,... | collective-permute-start | bytes 196616 | tf_op jit(solution)/shard_map/ppermute | solution.py:321
  68.7 10.5 %collective-permute-start.17 = (bf16[2,8,32,128]{3,2,1,0:T(8,128)(2,1)S(1)}, bf16[2,8,32,128]{3,2,1,0:T(8,128)(2,1)S(1)}, u32[]{:S(2)}, u32[]{:S(2)}) collective-permute-start(bf16[2,8,32,128]{3,2,1,0:T(8,128)(2,1)S(1)} %constant_dynamic-update-slice_fusion), channel_id=1, source_target_pairs={{0,2},{1,3},{2,0},{3,1},{4,6},{5,7},{6,4},{7,5},{8,10},{9,11},{10,... | collective-permute-start | bytes 393224 | tf_op jit(solution)/shard_map/ppermute | solution.py:321
  69.7 5.2 %collective-permute-start.11 = (bf16[1,8,32,128]{3,2,1,0:T(8,128)(2,1)S(1)}, bf16[1,8,32,128]{3,2,1,0:T(8,128)(2,1)S(1)}, u32[]{:S(2)}, u32[]{:S(2)}) collective-permute-start(bf16[1,8,32,128]{3,2,1,0:T(8,128)(2,1)S(1)} %slice.78), channel_id=1, source_target_pairs={{0,4},{1,5},{2,6},{3,7},{4,0},{5,1},{6,2},{7,3},{8,12},{9,13},{10,... | collective-permute-start | bytes 196616 | tf_op jit(solution)/shard_map/ppermute | solution.py:321
  70.4 6.6 %collective-permute-start.10 = (bf16[1,8,32,128]{3,2,1,0:T(8,128)(2,1)S(1)}, bf16[1,8,32,128]{3,2,1,0:T(8,128)(2,1)S(1)}, u32[]{:S(2)}, u32[]{:S(2)}) collective-permute-start(bf16[1,8,32,128]{3,2,1,0:T(8,128)(2,1)S(1)} %slice.76), channel_id=1, source_target_pairs={{0,4},{1,5},{2,6},{3,7},{4,0},{5,1},{6,2},{7,3},{8,12},{9,13},{10,... | collective-permute-start | bytes 196616 | tf_op jit(solution)/shard_map/ppermute | solution.py:321
  72.7 6.4 %collective-permute-start.18 = (bf16[2,8,32,128]{3,2,1,0:T(8,128)(2,1)S(1)}, bf16[2,8,32,128]{3,2,1,0:T(8,128)(2,1)S(1)}, u32[]{:S(2)}, u32[]{:S(2)}) collective-permute-start(bf16[2,8,32,128]{3,2,1,0:T(8,128)(2,1)S(1)} %constant_dynamic-update-slice_fusion.2), channel_id=1, source_target_pairs={{0,1},{1,0},{2,3},{3,2},{4,5},{5,4},{6,7},{7,6},{8,9},{9,8},{10,11... | collective-permute-start | bytes 393224 | tf_op jit(solution)/shard_map/ppermute | solution.py:321
  77.1 14.5 %copy-start.2 = (bf16[16,32,128]{2,1,0:T(8,128)(2,1)}, bf16[16,32,128]{2,1,0:T(8,128)(2,1)S(1)}, u32[]{:S(2)}) copy-start(bf16[16,32,128]{2,1,0:T(8,128)(2,1)S(1)} %pad_maximum_fusion.refs_0_) | copy-start | bytes 393220
  77.1 5.8 %collective-permute-start.16 = (bf16[16,32,128]{2,1,0:T(8,128)(2,1)S(1)}, bf16[16,32,128]{2,1,0:T(8,128)(2,1)S(1)}, u32[]{:S(2)}, u32[]{:S(2)}) collective-permute-start(bf16[16,32,128]{2,1,0:T(8,128)(2,1)S(1)} %pad_maximum_fusion.refs_0_), channel_id=1, source_target_pairs={{0,24},{8,16},{16,8},{24,0},{1,25},{9,17},{17,9},{25,1},{2,26},{10... | collective-permute-start | bytes 393224 | tf_op jit(solution)/shard_map/ppermute | solution.py:515
  77.2 8.6 %collective-permute-start.15 = (bf16[16,32,128]{2,1,0:T(8,128)(2,1)S(1)}, bf16[16,32,128]{2,1,0:T(8,128)(2,1)S(1)}, u32[]{:S(2)}, u32[]{:S(2)}) collective-permute-start(bf16[16,32,128]{2,1,0:T(8,128)(2,1)S(1)} %pad_maximum_fusion.refs_0_), channel_id=1, source_target_pairs={{0,16},{8,24},{16,0},{24,8},{1,17},{9,25},{17,1},{25,9},{2,18},{10... | collective-permute-start | bytes 393224 | tf_op jit(solution)/shard_map/ppermute | solution.py:515
  78.7 7.1 %collective-permute-start.14 = (bf16[16,32,128]{2,1,0:T(8,128)(2,1)S(1)}, bf16[16,32,128]{2,1,0:T(8,128)(2,1)S(1)}, u32[]{:S(2)}, u32[]{:S(2)}) collective-permute-start(bf16[16,32,128]{2,1,0:T(8,128)(2,1)S(1)} %pad_maximum_fusion.refs_0_), channel_id=1, source_target_pairs={{0,8},{8,0},{16,24},{24,16},{1,9},{9,1},{17,25},{25,17},{2,10},{10... | collective-permute-start | bytes 393224 | tf_op jit(solution)/shard_map/ppermute | solution.py:515
  79.1 21.7 %copy-start.1 = (bf16[4,8,32,128]{3,2,1,0:T(8,128)(2,1)}, bf16[4,8,32,128]{3,2,1,0:T(8,128)(2,1)S(1)}, u32[]{:S(2)}) copy-start(bf16[4,8,32,128]{3,2,1,0:T(8,128)(2,1)S(1)} %constant_dynamic-update-slice_fusion.6.refs_2_) | copy-start | bytes 786436
  79.1 21.6 %collective-permute-start.20 = (bf16[4,8,32,128]{3,2,1,0:T(8,128)(2,1)S(1)}, bf16[4,8,32,128]{3,2,1,0:T(8,128)(2,1)S(1)}, u32[]{:S(2)}, u32[]{:S(2)}) collective-permute-start(bf16[4,8,32,128]{3,2,1,0:T(8,128)(2,1)S(1)} %constant_dynamic-update-slice_fusion.6.refs_2_), channel_id=1, source_target_pairs={{0,2},{1,3},{2,0},{3,1},{4,6},{5,7},{6,4},{7,5},{8,10},{9,11},{10,... | collective-permute-start | bytes 786440 | tf_op jit(solution)/shard_map/ppermute | solution.py:321
  79.2 21.6 %copy-start = (bf16[4,8,32,128]{3,2,1,0:T(8,128)(2,1)}, bf16[4,8,32,128]{3,2,1,0:T(8,128)(2,1)S(1)}, u32[]{:S(2)}) copy-start(bf16[4,8,32,128]{3,2,1,0:T(8,128)(2,1)S(1)} %constant_dynamic-update-slice_fusion.4.refs_0_) | copy-start | bytes 786436
  79.2 21.5 %collective-permute-start.19 = (bf16[4,8,32,128]{3,2,1,0:T(8,128)(2,1)S(1)}, bf16[4,8,32,128]{3,2,1,0:T(8,128)(2,1)S(1)}, u32[]{:S(2)}, u32[]{:S(2)}) collective-permute-start(bf16[4,8,32,128]{3,2,1,0:T(8,128)(2,1)S(1)} %constant_dynamic-update-slice_fusion.4.refs_0_), channel_id=1, source_target_pairs={{0,1},{1,0},{2,3},{3,2},{4,5},{5,4},{6,7},{7,6},{8,9},{9,8},{10,11... | collective-permute-start | bytes 786440 | tf_op jit(solution)/shard_map/ppermute | solution.py:321
  81.6 9.9 %copy-start.3 = (bf16[16,32,128]{2,1,0:T(8,128)(2,1)}, bf16[16,32,128]{2,1,0:T(8,128)(2,1)S(1)}, u32[]{:S(2)}) copy-start(bf16[16,32,128]{2,1,0:T(8,128)(2,1)S(1)} %constant_dynamic-update-slice_fusion.8.refs_4_) | copy-start | bytes 393220
  82.9 8.6 %copy-start.8 = (bf16[16,32,128]{2,1,0:T(8,128)(2,1)}, bf16[16,32,128]{2,1,0:T(8,128)(2,1)S(1)}, u32[]{:S(2)}) copy-start(bf16[16,32,128]{2,1,0:T(8,128)(2,1)S(1)} %collective-permute-done.16.refs_3_) | copy-start | bytes 393220
  82.9 5.5 %collective-permute-start.23 = (bf16[16,32,128]{2,1,0:T(8,128)(2,1)S(1)}, bf16[16,32,128]{2,1,0:T(8,128)(2,1)S(1)}, u32[]{:S(2)}, u32[]{:S(2)}) collective-permute-start(bf16[16,32,128]{2,1,0:T(8,128)(2,1)S(1)} %constant_dynamic-update-slice_fusion.8.refs_4_), channel_id=1, source_target_pairs={{0,24},{8,16},{16,8},{24,0},{1,25},{9,17},{17,9},{25,1},{2,26},{10... | collective-permute-start | bytes 393224 | tf_op jit(solution)/shard_map/ppermute | solution.py:515
  85.8 5.8 %copy-start.9 = (bf16[16,32,128]{2,1,0:T(8,128)(2,1)}, bf16[16,32,128]{2,1,0:T(8,128)(2,1)S(1)}, u32[]{:S(2)}) copy-start(bf16[16,32,128]{2,1,0:T(8,128)(2,1)S(1)} %collective-permute-done.15.refs_2_) | copy-start | bytes 393220
  85.8 5.8 %collective-permute-start.22 = (bf16[16,32,128]{2,1,0:T(8,128)(2,1)S(1)}, bf16[16,32,128]{2,1,0:T(8,128)(2,1)S(1)}, u32[]{:S(2)}, u32[]{:S(2)}) collective-permute-start(bf16[16,32,128]{2,1,0:T(8,128)(2,1)S(1)} %constant_dynamic-update-slice_fusion.8.refs_4_), channel_id=1, source_target_pairs={{0,16},{8,24},{16,0},{24,8},{1,17},{9,25},{17,1},{25,9},{2,18},{10... | collective-permute-start | bytes 393224 | tf_op jit(solution)/shard_map/ppermute | solution.py:515
  85.8 5.8 %collective-permute-start.21 = (bf16[16,32,128]{2,1,0:T(8,128)(2,1)S(1)}, bf16[16,32,128]{2,1,0:T(8,128)(2,1)S(1)}, u32[]{:S(2)}, u32[]{:S(2)}) collective-permute-start(bf16[16,32,128]{2,1,0:T(8,128)(2,1)S(1)} %constant_dynamic-update-slice_fusion.8.refs_4_), channel_id=1, source_target_pairs={{0,8},{8,0},{16,24},{24,16},{1,9},{9,1},{17,25},{25,17},{2,10},{10... | collective-permute-start | bytes 393224 | tf_op jit(solution)/shard_map/ppermute | solution.py:515
  (8 other events, 13.0 us)

commit v2 on v1

--- a/solution.py
+++ b/solution.py
@@ -8,6 +8,7 @@
 from jax.experimental import pallas as pl
 from jax.experimental.pallas import tpu as pltpu
 from jax.sharding import PartitionSpec as P
+
 
 C = 64
 X = 64
@@ -147,6 +148,7 @@
 
 
 GROUP = 8
+QUAD = 4
 ROWS = 16
 LANES = 128
 BLOCK = 4
@@ -168,9 +170,10 @@
 
 def x_tables(length):
     cos_x, sin_x = angles_of(signed_waves(MX, length), length)
+    both = np.stack([cos_x, sin_x])
+    forward = np.einsum("qkx,cd->qkcdx", both, np.eye(QUAD))
+    forward = forward.reshape(2 * MX * QUAD, QUAD * length)
     unit = np.eye(GROUP)
-    both = np.stack([cos_x, sin_x])
-    forward = np.einsum("qkx,cd->qkcdx", both, unit).reshape(2 * MX * GROUP, GROUP * length)
     both = np.stack([cos_x, -sin_x])
     back = np.einsum("qkx,cd->dxqkc", both, unit).reshape(GROUP * length, 2 * MX * GROUP)
     return as_table(forward), as_table(back)
@@ -186,11 +189,17 @@
     back = np.concatenate(
         [np.concatenate([cos_z, sin_z], axis=1), np.concatenate([-sin_z, cos_z], axis=1)]
     )
-    return (
-        as_table(as_table(forward).astype(np.float32) * scale),
-        as_table(as_table(forward).astype(np.float32) * scale * doubled),
-        as_table(back * scale),
-    )
+    rounded = as_table(forward).astype(np.float32) * scale
+    return as_table(rounded.T), as_table((rounded * doubled).T), as_table(back * scale)
+
+
+def lane_table(waves, channels):
+    table = np.zeros((waves * channels, waves * channels))
+    for wave in range(waves):
+        for channel in range(channels):
+            group, place = divmod(channel, QUAD)
+            table[(group * waves + wave) * QUAD + place, wave * channels + channel] = 1.0
+    return as_table(table)
 
 
 def y_tables(length, shards):
@@ -224,97 +233,103 @@
     return lax.dot_general(left, right, dims, preferred_element_type=jnp.float32)
 
 
-def spectrum_kernel(
-    planes, orders, me_ref, field_ref, x_ref, z_ref, y_ref, *refs
-):
-    step = pl.program_id(0)
-    block, channels, length, depth = field_ref.shape[1:]
-    *part_refs, rows_ref, total_ref = refs
+def spectrum_kernel(block, orders, me_ref, field_ref, x_ref, z_ref, y_ref, lane_ref, *refs):
+    *part_refs, field_buf, rows_ref, total_ref, sems = refs
+    planes, channels, length, depth = field_buf.shape
     shards, _, width = total_ref.shape
-    for plane in range(block):
-        for first in range(0, channels, 2 * GROUP):
-            sides = [
-                field_ref[0, plane, first + side * GROUP : first + (side + 1) * GROUP].reshape(
-                    GROUP * length, depth
-                )
-                for side in range(2)
-            ]
-            mixed = dot(x_ref[...], jnp.concatenate(sides, axis=1))
-            half = MX * GROUP
-            parts = [
-                jnp.concatenate(
-                    [
-                        mixed[:half, side * depth : (side + 1) * depth],
-                        mixed[half:, side * depth : (side + 1) * depth],
-                    ],
-                    axis=1,
-                ).reshape(MX, GROUP, 2 * depth)
-                for side in range(2)
-            ]
-            rows_ref[plane, :, first : first + 2 * GROUP, :] = jnp.concatenate(
-                parts, axis=1
-            ).astype(jnp.bfloat16)
-        modes = dot(z_ref[...], rows_ref[plane].reshape(MX * channels, 2 * depth), 1, 1)
-        for shard in range(shards):
-            total_ref[shard, pl.ds(step * block + plane, 2 * MZ, stride=planes), :] = modes[
-                :, shard * width : (shard + 1) * width
-            ]
-
-    @pl.when(step == pl.num_programs(0) - 1)
-    def _():
-        me = me_ref[0]
-        table = y_ref[me]
-        chunk = MZ // len(orders)
-        for stream, order in enumerate(orders):
-            for kz in range(chunk):
-                first = (stream * chunk + kz) * planes
+
+    def incoming(plane):
+        return pltpu.make_async_copy(field_ref.at[0, plane], field_buf.at[plane], sems.at[plane])
+
+    for plane in range(planes):
+        incoming(plane).start()
+
+    @pl.loop(0, planes // block)
+    def _(step):
+        for place in range(block):
+            incoming(step * block + place).wait()
+        for place in range(block):
+            plane = step * block + place
+            for first in range(0, channels, 2 * QUAD):
+                sides = [
+                    field_buf[plane, first + side * QUAD : first + (side + 1) * QUAD].reshape(
+                        QUAD * length, depth
+                    )
+                    for side in range(2)
+                ]
+                mixed = dot(x_ref[...], jnp.concatenate(sides, axis=1))
+                half = MX * QUAD
                 parts = [
                     jnp.concatenate(
                         [
-                            total_ref[me ^ distance, pl.ds(part * MZ * planes + first, planes), :]
-                            for distance in order
+                            mixed[:half, side * depth : (side + 1) * depth],
+                            mixed[half:, side * depth : (side + 1) * depth],
                         ],
                         axis=1,
-                    )
-                    for part in range(2)
+                    ).reshape(shards, half // shards, 2 * depth)
+                    for side in range(2)
                 ]
-                modes = dot(table, jnp.concatenate(parts).astype(jnp.bfloat16))
-                modes = modes.astype(jnp.bfloat16)
-                for place in range(shards):
-                    side, place_in = divmod(place, shards // 2)
-                    part_refs[2 * stream + side][place_in, kz] = modes[
-                        :, place * width : (place + 1) * width
-                    ]
-
-
-def plane_modes(me, field, x_table, z_table, y_table, orders, block):
+                rows = half // shards
+                start = first // QUAD * rows
+                rows_ref[place, :, start : start + 2 * rows, :] = jnp.concatenate(
+                    parts, axis=1
+                ).astype(jnp.bfloat16)
+            for shard in range(shards):
+                modes = dot(rows_ref[place, shard], z_ref[...])
+                total_ref[shard, pl.ds(plane, 2 * MZ, stride=planes), :] = modes.T
+
+    me = me_ref[0]
+    table = y_ref[me]
+    chunk = MZ // len(orders)
+    for stream, order in enumerate(orders):
+        for kz in range(chunk):
+            first = (stream * chunk + kz) * planes
+            pieces = [
+                total_ref[me ^ distance, pl.ds(part * MZ * planes + first, planes), :]
+                for distance in order
+                for part in range(2)
+            ]
+            moved = jnp.concatenate(pieces).astype(jnp.bfloat16)
+            moved = dot(moved, lane_ref[...]).astype(jnp.bfloat16)
+            rows = 2 * planes
+            parts = [moved[place * rows : (place + 1) * rows] for place in range(shards)]
+            modes = dot(table, jnp.concatenate(parts, axis=1)).astype(jnp.bfloat16)
+            for place in range(shards):
+                side, place_in = divmod(place, shards // 2)
+                part_refs[2 * stream + side][place_in, kz] = modes[
+                    :, place * width : (place + 1) * width
+                ]
+
+
+def plane_modes(me, field, x_table, z_table, y_table, lanes, orders, block):
     _, planes, channels, length, depth = field.shape
     shards = len(orders[0])
     width = MX * channels // shards
     shape = (shards // 2, MZ // len(orders), 2 * MY, width)
-    whole = pl.BlockSpec(shape, lambda i: (0, 0, 0, 0))
+    vmem = pl.BlockSpec(memory_space=pltpu.VMEM)
     return pl.pallas_call(
-        functools.partial(spectrum_kernel, planes, orders),
+        functools.partial(spectrum_kernel, block, orders),
         out_shape=[jax.ShapeDtypeStruct(shape, jnp.bfloat16)] * (2 * len(orders)),
-        grid=(planes // block,),
         in_specs=[
             pl.BlockSpec(memory_space=pltpu.SMEM),
-            pl.BlockSpec((1, block, channels, length, depth), lambda i: (0, i, 0, 0, 0)),
-            pl.BlockSpec(x_table.shape, lambda i: (0, 0)),
-            pl.BlockSpec(z_table.shape, lambda i: (0, 0)),
-            pl.BlockSpec(y_table.shape, lambda i: (0, 0, 0)),
+            pl.BlockSpec(memory_space=pl.ANY),
+            vmem,
+            vmem,
+            vmem,
+            vmem,
         ],
-        out_specs=[whole] * (2 * len(orders)),
+        out_specs=[vmem] * (2 * len(orders)),
         scratch_shapes=[
-            pltpu.VMEM((block, MX, channels, 2 * depth), jnp.bfloat16),
+            pltpu.VMEM((planes, channels, length, depth), jnp.bfloat16),
+            pltpu.VMEM((block, shards, width, 2 * depth), jnp.bfloat16),
             pltpu.VMEM((shards, 2 * MZ * planes, width), jnp.float32),
+            pltpu.SemaphoreType.DMA((planes,)),
         ],
-        compiler_params=pltpu.CompilerParams(dimension_semantics=("arbitrary",)),
         cost_estimate=pl.CostEstimate(
             flops=2 * field.size * 8 * MX, bytes_accessed=2 * field.size, transcendentals=0
         ),
         name="plane_modes",
-    )(me, field, x_table, z_table, y_table)
+    )(me, field, x_table, z_table, y_table, lanes)
 
 
 def swapped(array, bit, shards):
@@ -348,7 +363,8 @@
     return jnp.where(low, pltpu.roll(plain, LANES // 2, 1), turned)
 
 
-def mode_grad_kernel(keep_ref, moved_ref, w_ref, modes_ref, grad_ref):
+def mode_grad_kernel(keep_ref, moved_ref, w_ref, *refs):
+    *_, modes_ref, grad_ref = refs
     _, chunk, _, channels, _ = w_ref.shape
     row = lax.broadcasted_iota(jnp.int32, (2 * MY, MY * channels), 0) // 2
     lane = lax.broadcasted_iota(jnp.int32, (2 * MY, MY * channels), 1) // channels
@@ -370,14 +386,14 @@
         grad_ref[0, kz] = jnp.where(low, sides[0], sides[1]).astype(jnp.bfloat16)
 
 
-def mode_grads(keep, moved, weights, first, chunk):
+def mode_grads(keep, moved, weights, modes, first, chunk):
     _, kinds, rows, width = keep.shape
     channels = weights.shape[3]
     part_spec = pl.BlockSpec((1, chunk, rows, width), lambda i: (0, i, 0, 0))
     return pl.pallas_call(
         mode_grad_kernel,
         out_shape=(
-            jax.ShapeDtypeStruct(keep.shape[1:], jnp.bfloat16),
+            jax.ShapeDtypeStruct((MZ, rows, width), jnp.bfloat16),
             jax.ShapeDtypeStruct(keep.shape, jnp.bfloat16),
         ),
         grid=(kinds // chunk,),
@@ -387,14 +403,19 @@
             pl.BlockSpec(
                 (2, chunk, MY, channels, 2 * channels), lambda i: (0, i + first // chunk, 0, 0, 0)
             ),
-        ],
-        out_specs=(pl.BlockSpec((chunk, rows, width), lambda i: (i, 0, 0)), part_spec),
+        ]
+        + [pl.BlockSpec(memory_space=pl.ANY)] * len(modes),
+        out_specs=(
+            pl.BlockSpec((chunk, rows, width), lambda i: (i + first // chunk, 0, 0)),
+            part_spec,
+        ),
+        input_output_aliases={3: 0} if modes else {},
         compiler_params=pltpu.CompilerParams(dimension_semantics=("arbitrary",)),
         cost_estimate=pl.CostEstimate(
             flops=4 * MY * weights.size, bytes_accessed=weights.size, transcendentals=0
         ),
         name="mode_grads",
-    )(keep, moved, weights)
+    )(keep, moved, weights, *modes)
 
 
 def weight_kernel(channels, *refs):
@@ -445,13 +466,14 @@
         me = me_ref[0]
         table = y_ref[me]
         chunk = MZ // len(orders)
+        count = len(held_refs) // len(orders)
         for stream, order in enumerate(orders):
             for kz in range(chunk):
                 modes = jnp.concatenate(
                     [
                         ref[place, kz]
-                        for ref in held_refs[2 * stream : 2 * stream + 2]
-                        for place in range(shards // 2)
+                        for ref in held_refs[stream * count : (stream + 1) * count]
+                        for place in range(ref.shape[0])
                     ],
                     axis=1,
                 )
@@ -511,10 +533,11 @@
 
 
 def from_peers(array, groups):
-    others = [
-        lax.ppermute(array, "batch", [(i, i ^ k) for i in range(groups)]) for k in range(1, groups)
-    ]
-    return [array] + others
+    held = [array]
+    for bit in [1 << place for place in range(groups.bit_length() - 1)][::-1]:
+        pairs = [(i, i ^ bit) for i in range(groups)]
+        held = held + [lax.ppermute(one, "batch", pairs) for one in held]
+    return held
 
 
 def local_fast(shards, groups, inputs, cotangent, mode_weights):
@@ -523,6 +546,7 @@
     x_table, x_back = x_tables(length)
     z_plain, z_double, z_back = z_tables(depth, scale)
     y_table, y_back = y_tables(planes * shards, shards)
+    lanes = lane_table(MX // shards, channels)
     me = lax.axis_index("space").reshape(1)
     bits = [1 << place for place in range(shards.bit_length() - 1)]
     paths = [bits, [bits[1], bits[0]] + bits[2:]]
@@ -538,11 +562,14 @@
         return [pair[0] for pair in pairs], [pair[1] for pair in pairs]
 
     def swap_all(arrays, routes, step):
-        return [swapped(arrays[k], routes[k][step], shards) for k in streams]
-
-    keep, send = split(plane_modes(me, cotangent, x_table, z_double, y_table, down, BLOCK))
+        moved = []
+        for k in streams:
+            moved.append(swapped(arrays[k], routes[k][step], shards))
+        return moved
+
+    keep, send = split(plane_modes(me, cotangent, x_table, z_double, y_table, lanes, down, BLOCK))
     moved = swap_all(send, paths, 0)
-    parts = plane_modes(me, inputs, x_table, z_plain, y_table, down, BLOCK)
+    parts = plane_modes(me, inputs, x_table, z_plain, y_table, lanes, down, BLOCK)
     moved, parts = after((moved, parts))
     input_keep, input_send = split(parts)
     input_moved, input_sends = None, 0
@@ -558,38 +585,30 @@
         input_sends += 1
     weights = mode_weights.reshape(2, MZ, MY, channels, 2 * channels)
     chunk = MZ // len(paths)
-    cot_modes, held = [], []
+    routes = [path[::-1] for path in paths]
+    cot_modes, held, came = [], [], []
     for k in streams:
         if k:
-            keep[k], cot_modes[-1] = after((keep[k], cot_modes[-1]))
-        else:
-            keep[k], input_send = after((keep[k], input_send))
-        modes, grad = mode_grads(keep[k], moved[k], weights, k * chunk, STEP)
-        cot_modes.append(modes)
-        held.append(grad)
-    routes = [path[::-1] for path in paths]
-    came = swap_all(held, routes, 0)
-    while input_sends < len(bits):
-        input_moved, cot_modes[-1] = after((input_moved, cot_modes[-1]))
-        input_keep, input_send = reduce_step(input_keep, input_moved)
-        input_moved = swap_all(input_send, paths, input_sends)
-        input_sends += 1
-    all_cots = from_peers(jnp.concatenate(cot_modes), groups)
-    input_modes = None
+            input_keep, input_send = reduce_step(input_keep, input_moved)
+            input_moved = swap_all(input_send, paths, input_sends)
+        keep[k], input_send = after((keep[k], input_send))
+        modes, grad = mode_grads(keep[k], moved[k], weights, cot_modes, k * chunk, STEP)
+        cot_modes = [modes]
+        held.append([grad])
+        came.append(swapped(grad, routes[k][0], shards))
+    input_modes = jnp.concatenate([total(input_keep[k][0], input_moved[k][0]) for k in streams])
+    input_modes, came = after((input_modes, came))
+    all_cots = from_peers(cot_modes[0], groups)
+    all_inputs = from_peers(input_modes, groups)
+    came = [[array] for array in came]
     for step in range(1, len(bits)):
-        held = [jnp.concatenate([held[k], came[k]]) for k in streams]
-        came = swap_all(held, routes, step)
-        if step == 1:
-            input_moved, held = after((input_moved, held))
-            input_modes = jnp.concatenate([total(input_keep[k][0], input_moved[k][0]) for k in streams])
-            all_inputs = from_peers(input_modes, groups)
+        held = [[jnp.concatenate(held[k] + came[k])] for k in streams]
+        came = [[array] for array in swap_all([one[0] for one in held], routes, step)]
     all_inputs, held = after((all_inputs, held))
     weight_grad = weight_grads(all_inputs, all_cots, channels, STEP)
     came, weight_grad = after((came, weight_grad))
-    gathered = [array for k in streams for array in (held[k], came[k])]
-    input_grad = plane_grads(
-        me, gathered, y_back, z_back, x_back, up, inputs.shape, BLOCK
-    )
+    gathered = [array for k in streams for array in held[k] + came[k]]
+    input_grad = plane_grads(me, gathered, y_back, z_back, x_back, up, inputs.shape, BLOCK)
     return (input_grad, weight_grad.reshape(mode_weights.shape))
 
 

time: 118 us -> 110 us (0.932)
  waiting for transfers between devices: 21.4 us -> 15.1 us
  local copies, waits for them, and re-layouts: 8.81 us -> 6.88 us
  Pallas kernels: 58.1 us -> 56.2 us
  other arithmetic: 2.4 us -> 4.1 us
    ppermute x6, waiting for transfers between devices: 9.46 us -> 1.28 us  [from_peers(): held = held + [lax.ppermute(one, 'batch', pairs) for one in held]]
    pallas_call x4, Pallas kernels: 34.8 us -> 32.9 us  [the longest x2 24.6 us: plane_modes(): pl.pallas_call(functools.partial(spectrum_kernel, block, orders), out_sha...]
    ppermute x18, waiting for transfers between devices: 12 us -> 13.8 us  [swapped(): return lax.ppermute(array, 'space', [(i, i ^ bit) for i in range(shards)])]
    concatenate x0 -> x2, other arithmetic: none -> 1.71 us  [local_fast(): held = [[jnp.concatenate(held[k] + came[k])] for k in streams]]
    ppermute x18, starting transfers between devices: 23.6 us -> 22.2 us  [swapped(): return lax.ppermute(array, 'space', [(i, i ^ bit) for i in range(shards)])]
    ppermute x6, starting transfers between devices: 2.33 us -> 3.55 us  [from_peers(): held = held + [lax.ppermute(one, 'batch', pairs) for one in held]]
    unnamed x37 -> x34, local copies, waits for them, and re-layouts: 6.56 us -> 5.52 us
  transfers between devices with their start and end apart: 24 -> 24, of which waited for: 12 -> 10; matrix products, arithmetic and copies ran while one was open for 6% -> 6% of each run, Pallas kernels for 25% -> 26%
where the time goes in v2:
time: 110 us; the launch traced here: 109 us
  Pallas kernels  56.2 us (51%)
  starting transfers between devices  25.8 us (23%)
  waiting for transfers between devices  15.1 us (14%)
  local copies, waits for them, and re-layouts  6.88 us (6%)
  other arithmetic  4.1 us (4%)
    pallas_call x2, Pallas kernels, plane_modes(): pl.pallas_call(functools.partial(spectrum_kernel, block, orders), out_sha...  24.6 us
    ppermute x18, starting transfers between devices, swapped(): return lax.ppermute(array, 'space', [(i, i ^ bit) for i in range(shards)])  22.2 us
    pallas_call x1, Pallas kernels, plane_grads(): pl.pallas_call(functools.partial(inverse_kernel, orders), out_shape=jax.S...  15.4 us
    ppermute x18, waiting for transfers between devices, swapped(): return lax.ppermute(array, 'space', [(i, i ^ bit) for i in range(shards)])  13.8 us
    pallas_call x2, Pallas kernels, mode_grads(): pl.pallas_call(mode_grad_kernel, out_shape=(jax.ShapeDtypeStruct((MZ, row...  8.24 us
    pallas_call x1, Pallas kernels, weight_grads(): pl.pallas_call(functools.partial(weight_kernel, channels), out_shape=jax....  7.88 us
    unnamed x34, local copies, waits for them, and re-layouts  5.52 us
    ppermute x6, starting transfers between devices, from_peers(): held = held + [lax.ppermute(one, 'batch', pairs) for one in held]  3.55 us
  transfers between devices with their start and end apart: 24, of which 10 were waited for; matrix products, arithmetic and copies ran while one was open for 6% of the time, Pallas kernels for 26%

profile of v2, /device:TPU:0, one launch (start us, length us, event | category | flops | bytes accessed | tf_op | source)
XLA Modules:
  0.0 109.0 jit_solution(18150270757569684238)
XLA Ops:
  0.6 12.3 %plane_modes.2 = (bf16[4,8,32,128]{3,2,1,0:T(8,128)(2,1)}, bf16[4,8,32,128]{3,2,1,0:T(8,128)(2,1)}, bf16[4,8,32,128]{3,2,1,0:T(8,128)(2,1)}, bf16[4,8,32,128]{3,2,1,0:T(8,128)(2,1)}) custom-call(s32[1]{0:T(128)} %bitcast.me_ref, bf16[1,16,64,64,128]{4,3,2,1,0:T(8,128)(2,1)} %field_ref.2, bf16[128,256]{1,0:T(8,128)(2,1)} %constant.20.clone.x_ref, ...), custom_call_target="tpu_custom_call" | custom-call | flops 2147483648 | bytes 16777216 | tf_op jit(solution)/shard_map/plane_modes/pallas_call | solution.py:310
  13.0 3.1 %collective-permute-start = (bf16[4,8,32,128]{3,2,1,0:T(8,128)(2,1)}, bf16[4,8,32,128]{3,2,1,0:T(8,128)(2,1)S(1)}, u32[]{:S(2)}, u32[]{:S(2)}) collective-permute-start(bf16[4,8,32,128]{3,2,1,0:T(8,128)(2,1)} %get-tuple-element.42), channel_id=1, source_target_pairs={{0,1},{1,0},{2,3},{3,2},{4,5},{5,4},{6,7},{7,6},{8,9},{9,8},{10,11... | collective-permute-start | bytes 786440 | tf_op jit(solution)/shard_map/ppermute | solution.py:336
  16.0 1.6 %collective-permute-start.1 = (bf16[4,8,32,128]{3,2,1,0:T(8,128)(2,1)}, bf16[4,8,32,128]{3,2,1,0:T(8,128)(2,1)S(1)}, u32[]{:S(2)}, u32[]{:S(2)}) collective-permute-start(bf16[4,8,32,128]{3,2,1,0:T(8,128)(2,1)} %get-tuple-element.43), channel_id=1, source_target_pairs={{0,2},{1,3},{2,0},{3,1},{4,6},{5,7},{6,4},{7,5},{8,10},{9,11},{10,... | collective-permute-start | bytes 786440 | tf_op jit(solution)/shard_map/ppermute | solution.py:336
  17.6 12.3 %plane_modes.3 = (bf16[4,8,32,128]{3,2,1,0:T(8,128)(2,1)}, bf16[4,8,32,128]{3,2,1,0:T(8,128)(2,1)}, bf16[4,8,32,128]{3,2,1,0:T(8,128)(2,1)}, bf16[4,8,32,128]{3,2,1,0:T(8,128)(2,1)}) custom-call(s32[1]{0:T(128)} %bitcast.me_ref, bf16[1,16,64,64,128]{4,3,2,1,0:T(8,128)(2,1)} %field_ref.3, bf16[128,256]{1,0:T(8,128)(2,1)} %constant.20.clone.x_ref, ...), custom_call_target="tpu_custom_call" | custom-call | flops 2147483648 | bytes 16777216 | tf_op jit(solution)/shard_map/plane_modes/pallas_call | solution.py:310
  30.8 1.9 %collective-permute-start.4 = (bf16[4,8,32,128]{3,2,1,0:T(8,128)(2,1)}, bf16[4,8,32,128]{3,2,1,0:T(8,128)(2,1)S(1)}, u32[]{:S(2)}, u32[]{:S(2)}) collective-permute-start(bf16[4,8,32,128]{3,2,1,0:T(8,128)(2,1)} %get-tuple-element.57), channel_id=1, source_target_pairs={{0,1},{1,0},{2,3},{3,2},{4,5},{5,4},{6,7},{7,6},{8,9},{9,8},{10,11... | collective-permute-start | bytes 786440 | tf_op jit(solution)/shard_map/ppermute | solution.py:336
  32.7 1.6 %collective-permute-start.5 = (bf16[4,8,32,128]{3,2,1,0:T(8,128)(2,1)}, bf16[4,8,32,128]{3,2,1,0:T(8,128)(2,1)S(1)}, u32[]{:S(2)}, u32[]{:S(2)}) collective-permute-start(bf16[4,8,32,128]{3,2,1,0:T(8,128)(2,1)} %get-tuple-element.58), channel_id=1, source_target_pairs={{0,2},{1,3},{2,0},{3,1},{4,6},{5,7},{6,4},{7,5},{8,10},{9,11},{10,... | collective-permute-start | bytes 786440 | tf_op jit(solution)/shard_map/ppermute | solution.py:336
  34.3 2.2 %collective-permute-done.2 = bf16[2,8,32,128]{3,2,1,0:T(8,128)(2,1)S(1)} collective-permute-done((bf16[2,8,32,128]{3,2,1,0:T(8,128)(2,1)S(1)}, bf16[2,8,32,128]{3,2,1,0:T(8,128)(2,1)S(1)}, u32[]{:S(2)}, u32[]{:S(2)}) %collective-permute-start.2) | collective-permute-done | bytes 131104 | tf_op jit(solution)/shard_map/ppermute | solution.py:336
  37.1 0.6 fusion.3
  38.4 2.3 %collective-permute-done.4 = bf16[4,8,32,128]{3,2,1,0:T(8,128)(2,1)S(1)} collective-permute-done((bf16[4,8,32,128]{3,2,1,0:T(8,128)(2,1)}, bf16[4,8,32,128]{3,2,1,0:T(8,128)(2,1)S(1)}, u32[]{:S(2)}, u32[]{:S(2)}) %collective-permute-start.4) | collective-permute-done | bytes 262176 | tf_op jit(solution)/shard_map/ppermute | solution.py:336
  40.8 2.6 %collective-permute-start.10 = (bf16[1,8,32,128]{3,2,1,0:T(8,128)(2,1)S(1)}, bf16[1,8,32,128]{3,2,1,0:T(8,128)(2,1)S(1)}, u32[]{:S(2)}, u32[]{:S(2)}) collective-permute-start(bf16[1,8,32,128]{3,2,1,0:T(8,128)(2,1)S(1)} %get-tuple-element.63), channel_id=1, source_target_pairs={{0,4},{1,5},{2,6},{3,7},{4,0},{5,1},{6,2},{7,3},{8,12},{9,13},{10,... | collective-permute-start | bytes 196616 | tf_op jit(solution)/shard_map/ppermute | solution.py:336
  43.8 1.0 add_convert_fusion.1
  44.8 1.0 add_convert_fusion
  45.8 1.5 %collective-permute-start.6 = (bf16[2,8,32,128]{3,2,1,0:T(8,128)(2,1)S(1)}, bf16[2,8,32,128]{3,2,1,0:T(8,128)(2,1)S(1)}, u32[]{:S(2)}, u32[]{:S(2)}) collective-permute-start(bf16[2,8,32,128]{3,2,1,0:T(8,128)(2,1)S(1)} %slice.71), channel_id=1, source_target_pairs={{0,2},{1,3},{2,0},{3,1},{4,6},{5,7},{6,4},{7,5},{8,10},{9,11},{10,... | collective-permute-start | bytes 393224 | tf_op jit(solution)/shard_map/ppermute | solution.py:336
  48.7 4.1 %mode_grads.2 = (bf16[16,32,128]{2,1,0:T(8,128)(2,1)}, bf16[1,8,32,128]{3,2,1,0:T(8,128)(2,1)}) custom-call(bf16[1,8,32,128]{3,2,1,0:T(8,128)(2,1)} %get-tuple-element.62.keep_ref, bf16[1,8,32,128]{3,2,1,0:T(8,128)(2,1)} %copy-done.14, bf16[2,16,16,64,128]{4,3,2,1,0:T(8,128)(2,1)} %bitcast.7), custom_call_target="tpu_custom_call" | custom-call | flops 268435456 | bytes 4194304 | tf_op jit(solution)/shard_map/mode_grads/pallas_call | solution.py:393
  52.8 2.5 %collective-permute-start.11 = (bf16[1,8,32,128]{3,2,1,0:T(8,128)(2,1)}, bf16[1,8,32,128]{3,2,1,0:T(8,128)(2,1)S(1)}, u32[]{:S(2)}, u32[]{:S(2)}) collective-permute-start(bf16[1,8,32,128]{3,2,1,0:T(8,128)(2,1)} %get-tuple-element.64), channel_id=1, source_target_pairs={{0,4},{1,5},{2,6},{3,7},{4,0},{5,1},{6,2},{7,3},{8,12},{9,13},{10,... | collective-permute-start | bytes 196616 | tf_op jit(solution)/shard_map/ppermute | solution.py:336
  55.3 0.9 constant_dynamic-update-slice_fusion.2
  56.8 2.5 %collective-permute-start.9 = (bf16[1,8,32,128]{3,2,1,0:T(8,128)(2,1)S(1)}, bf16[1,8,32,128]{3,2,1,0:T(8,128)(2,1)S(1)}, u32[]{:S(2)}, u32[]{:S(2)}) collective-permute-start(bf16[1,8,32,128]{3,2,1,0:T(8,128)(2,1)S(1)} %slice.77), channel_id=1, source_target_pairs={{0,4},{1,5},{2,6},{3,7},{4,0},{5,1},{6,2},{7,3},{8,12},{9,13},{10,... | collective-permute-start | bytes 196616 | tf_op jit(solution)/shard_map/ppermute | solution.py:336
  59.9 4.1 %mode_grads.3 = (bf16[16,32,128]{2,1,0:T(8,128)(2,1)}, bf16[1,8,32,128]{3,2,1,0:T(8,128)(2,1)}) custom-call(bf16[1,8,32,128]{3,2,1,0:T(8,128)(2,1)} %get-tuple-element.65.keep_ref, bf16[1,8,32,128]{3,2,1,0:T(8,128)(2,1)} %copy-done.13, bf16[2,16,16,64,128]{4,3,2,1,0:T(8,128)(2,1)} %bitcast.8, ...), custom_call_target="tpu_custom_call", output_to_operand_aliasing={{0}: (3, {})} | custom-call | flops 268435456 | bytes 4194304 | tf_op jit(solution)/shard_map/mode_grads/pallas_call | solution.py:393
  64.5 1.5 %collective-permute-start.21 = (bf16[16,32,128]{2,1,0:T(8,128)(2,1)}, bf16[16,32,128]{2,1,0:T(8,128)(2,1)S(1)}, u32[]{:S(2)}, u32[]{:S(2)}) collective-permute-start(bf16[16,32,128]{2,1,0:T(8,128)(2,1)} %get-tuple-element.77.refs_4_), channel_id=1, source_target_pairs={{0,16},{8,24},{16,0},{24,8},{1,17},{9,25},{17,1},{25,9},{2,18},{10... | collective-permute-start | bytes 393224 | tf_op jit(solution)/shard_map/ppermute | solution.py:539
  66.0 0.8 constant_dynamic-update-slice_fusion.5
  67.0 3.2 %collective-permute-done.13 = bf16[1,8,32,128]{3,2,1,0:T(8,128)(2,1)S(1)} collective-permute-done((bf16[1,8,32,128]{3,2,1,0:T(8,128)(2,1)}, bf16[1,8,32,128]{3,2,1,0:T(8,128)(2,1)S(1)}, u32[]{:S(2)}, u32[]{:S(2)}) %collective-permute-start.13) | collective-permute-done | bytes 65568 | tf_op jit(solution)/shard_map/ppermute | solution.py:336
  70.1 1.5 %collective-permute-start.14 = (bf16[16,32,128]{2,1,0:T(8,128)(2,1)S(1)}, bf16[16,32,128]{2,1,0:T(8,128)(2,1)S(1)}, u32[]{:S(2)}, u32[]{:S(2)}) collective-permute-start(bf16[16,32,128]{2,1,0:T(8,128)(2,1)S(1)} %pad_maximum_fusion.refs_0_), channel_id=1, source_target_pairs={{0,16},{8,24},{16,0},{24,8},{1,17},{9,25},{17,1},{25,9},{2,18},{10... | collective-permute-start | bytes 393224 | tf_op jit(solution)/shard_map/ppermute | solution.py:539
  71.6 0.9 pad_maximum_fusion.1
  72.5 0.9 pad_maximum_fusion.2
  73.3 1.5 %collective-permute-start.18 = (bf16[2,8,32,128]{3,2,1,0:T(8,128)(2,1)S(1)}, bf16[2,8,32,128]{3,2,1,0:T(8,128)(2,1)S(1)}, u32[]{:S(2)}, u32[]{:S(2)}) collective-permute-start(bf16[2,8,32,128]{3,2,1,0:T(8,128)(2,1)S(1)} %pad_maximum_fusion.2), channel_id=1, source_target_pairs={{0,1},{1,0},{2,3},{3,2},{4,5},{5,4},{6,7},{7,6},{8,9},{9,8},{10,11... | collective-permute-start | bytes 393224 | tf_op jit(solution)/shard_map/ppermute | solution.py:336
  74.9 5.3 %collective-permute-done.17 = bf16[2,8,32,128]{3,2,1,0:T(8,128)(2,1)S(1)} collective-permute-done((bf16[2,8,32,128]{3,2,1,0:T(8,128)(2,1)S(1)}, bf16[2,8,32,128]{3,2,1,0:T(8,128)(2,1)S(1)}, u32[]{:S(2)}, u32[]{:S(2)}) %collective-permute-start.17) | collective-permute-done | bytes 131104 | tf_op jit(solution)/shard_map/ppermute | solution.py:336
  81.9 0.7 collective-permute-done.16.refs_3_
  83.6 0.6 copy-done.12
  84.3 7.9 %weight_grads.1 = f32[2,16,16,64,128]{4,3,2,1,0:T(8,128)} custom-call(bf16[16,32,128]{2,1,0:T(8,128)(2,1)} %copy-done, bf16[16,32,128]{2,1,0:T(8,128)(2,1)} %copy-done.9, bf16[16,32,128]{2,1,0:T(8,128)(2,1)} %copy-done.8, bf16[16,32,128]{2,1,0:T(8,128)(2,1)} %copy-done.10, bf16[16,32,128]{2,1,0:T(8,128)(2,1)} %get-tuple-element.77.refs_4_, ...), custom_call_target="tpu_custom_call" | custom-call | flops 1073741824 | bytes 16777216 | tf_op jit(solution)/shard_map/weight_grads/pallas_call | solution.py:444
  92.2 0.7 copy-done.3
  92.9 0.7 copy-done.4
  93.6 15.4 %plane_grads.1 = bf16[1,16,64,64,128]{4,3,2,1,0:T(8,128)(2,1)} custom-call(s32[1]{0:T(128)} %bitcast.me_ref, bf16[4,8,32,128]{3,2,1,0:T(8,128)(2,1)} %copy-done.1, bf16[4,8,32,128]{3,2,1,0:T(8,128)(2,1)} %copy-done.3, bf16[4,8,32,128]{3,2,1,0:T(8,128)(2,1)} %copy-done.2, bf16[4,8,32,128]{3,2,1,0:T(8,128)(2,1)} %copy-done.4, ...), custom_call_target="tpu_custom_call" | custom-call | flops 2147483648 | bytes 16777216 | tf_op jit(solution)/shard_map/plane_grads/pallas_call | solution.py:512
  (78 shorter events, 8.3 us)
Async XLA Ops:
  12.9 17.0 %copy-start.5 = (bf16[4,8,32,128]{3,2,1,0:T(8,128)(2,1)S(1)}, bf16[4,8,32,128]{3,2,1,0:T(8,128)(2,1)}, u32[]{:S(2)}) copy-start(bf16[4,8,32,128]{3,2,1,0:T(8,128)(2,1)} %get-tuple-element.49) | copy-start | bytes 786436
  13.0 17.0 %copy-start.6 = (bf16[4,8,32,128]{3,2,1,0:T(8,128)(2,1)S(1)}, bf16[4,8,32,128]{3,2,1,0:T(8,128)(2,1)}, u32[]{:S(2)}) copy-start(bf16[4,8,32,128]{3,2,1,0:T(8,128)(2,1)} %get-tuple-element.51) | copy-start | bytes 786436
  13.0 17.0 %collective-permute-start = (bf16[4,8,32,128]{3,2,1,0:T(8,128)(2,1)}, bf16[4,8,32,128]{3,2,1,0:T(8,128)(2,1)S(1)}, u32[]{:S(2)}, u32[]{:S(2)}) collective-permute-start(bf16[4,8,32,128]{3,2,1,0:T(8,128)(2,1)} %get-tuple-element.42), channel_id=1, source_target_pairs={{0,1},{1,0},{2,3},{3,2},{4,5},{5,4},{6,7},{7,6},{8,9},{9,8},{10,11... | collective-permute-start | bytes 786440 | tf_op jit(solution)/shard_map/ppermute | solution.py:336
  16.0 13.9 %collective-permute-start.1 = (bf16[4,8,32,128]{3,2,1,0:T(8,128)(2,1)}, bf16[4,8,32,128]{3,2,1,0:T(8,128)(2,1)S(1)}, u32[]{:S(2)}, u32[]{:S(2)}) collective-permute-start(bf16[4,8,32,128]{3,2,1,0:T(8,128)(2,1)} %get-tuple-element.43), channel_id=1, source_target_pairs={{0,2},{1,3},{2,0},{3,1},{4,6},{5,7},{6,4},{7,5},{8,10},{9,11},{10,... | collective-permute-start | bytes 786440 | tf_op jit(solution)/shard_map/ppermute | solution.py:336
  30.2 6.3 %collective-permute-start.2 = (bf16[2,8,32,128]{3,2,1,0:T(8,128)(2,1)S(1)}, bf16[2,8,32,128]{3,2,1,0:T(8,128)(2,1)S(1)}, u32[]{:S(2)}, u32[]{:S(2)}) collective-permute-start(bf16[2,8,32,128]{3,2,1,0:T(8,128)(2,1)S(1)} %slice.65), channel_id=1, source_target_pairs={{0,2},{1,3},{2,0},{3,1},{4,6},{5,7},{6,4},{7,5},{8,10},{9,11},{10,... | collective-permute-start | bytes 393224 | tf_op jit(solution)/shard_map/ppermute | solution.py:336
  30.7 6.4 %collective-permute-start.3 = (bf16[2,8,32,128]{3,2,1,0:T(8,128)(2,1)S(1)}, bf16[2,8,32,128]{3,2,1,0:T(8,128)(2,1)S(1)}, u32[]{:S(2)}, u32[]{:S(2)}) collective-permute-start(bf16[2,8,32,128]{3,2,1,0:T(8,128)(2,1)S(1)} %slice.66), channel_id=1, source_target_pairs={{0,1},{1,0},{2,3},{3,2},{4,5},{5,4},{6,7},{7,6},{8,9},{9,8},{10,11... | collective-permute-start | bytes 393224 | tf_op jit(solution)/shard_map/ppermute | solution.py:336
  30.8 9.9 %collective-permute-start.4 = (bf16[4,8,32,128]{3,2,1,0:T(8,128)(2,1)}, bf16[4,8,32,128]{3,2,1,0:T(8,128)(2,1)S(1)}, u32[]{:S(2)}, u32[]{:S(2)}) collective-permute-start(bf16[4,8,32,128]{3,2,1,0:T(8,128)(2,1)} %get-tuple-element.57), channel_id=1, source_target_pairs={{0,1},{1,0},{2,3},{3,2},{4,5},{5,4},{6,7},{7,6},{8,9},{9,8},{10,11... | collective-permute-start | bytes 786440 | tf_op jit(solution)/shard_map/ppermute | solution.py:336
  32.7 8.1 %collective-permute-start.5 = (bf16[4,8,32,128]{3,2,1,0:T(8,128)(2,1)}, bf16[4,8,32,128]{3,2,1,0:T(8,128)(2,1)S(1)}, u32[]{:S(2)}, u32[]{:S(2)}) collective-permute-start(bf16[4,8,32,128]{3,2,1,0:T(8,128)(2,1)} %get-tuple-element.58), channel_id=1, source_target_pairs={{0,2},{1,3},{2,0},{3,1},{4,6},{5,7},{6,4},{7,5},{8,10},{9,11},{10,... | collective-permute-start | bytes 786440 | tf_op jit(solution)/shard_map/ppermute | solution.py:336
  40.8 7.2 %collective-permute-start.10 = (bf16[1,8,32,128]{3,2,1,0:T(8,128)(2,1)S(1)}, bf16[1,8,32,128]{3,2,1,0:T(8,128)(2,1)S(1)}, u32[]{:S(2)}, u32[]{:S(2)}) collective-permute-start(bf16[1,8,32,128]{3,2,1,0:T(8,128)(2,1)S(1)} %get-tuple-element.63), channel_id=1, source_target_pairs={{0,4},{1,5},{2,6},{3,7},{4,0},{5,1},{6,2},{7,3},{8,12},{9,13},{10,... | collective-permute-start | bytes 196616 | tf_op jit(solution)/shard_map/ppermute | solution.py:336
  43.4 15.9 %collective-permute-start.12 = (bf16[1,8,32,128]{3,2,1,0:T(8,128)(2,1)S(1)}, bf16[1,8,32,128]{3,2,1,0:T(8,128)(2,1)S(1)}, u32[]{:S(2)}, u32[]{:S(2)}) collective-permute-start(bf16[1,8,32,128]{3,2,1,0:T(8,128)(2,1)S(1)} %get-tuple-element.66), channel_id=1, source_target_pairs={{0,4},{1,5},{2,6},{3,7},{4,0},{5,1},{6,2},{7,3},{8,12},{9,13},{10,... | collective-permute-start | bytes 196616 | tf_op jit(solution)/shard_map/ppermute | solution.py:336
  45.8 10.3 %collective-permute-start.6 = (bf16[2,8,32,128]{3,2,1,0:T(8,128)(2,1)S(1)}, bf16[2,8,32,128]{3,2,1,0:T(8,128)(2,1)S(1)}, u32[]{:S(2)}, u32[]{:S(2)}) collective-permute-start(bf16[2,8,32,128]{3,2,1,0:T(8,128)(2,1)S(1)} %slice.71), channel_id=1, source_target_pairs={{0,2},{1,3},{2,0},{3,1},{4,6},{5,7},{6,4},{7,5},{8,10},{9,11},{10,... | collective-permute-start | bytes 393224 | tf_op jit(solution)/shard_map/ppermute | solution.py:336
  47.4 9.3 %collective-permute-start.8 = (bf16[2,8,32,128]{3,2,1,0:T(8,128)(2,1)S(1)}, bf16[2,8,32,128]{3,2,1,0:T(8,128)(2,1)S(1)}, u32[]{:S(2)}, u32[]{:S(2)}) collective-permute-start(bf16[2,8,32,128]{3,2,1,0:T(8,128)(2,1)S(1)} %slice.75), channel_id=1, source_target_pairs={{0,1},{1,0},{2,3},{3,2},{4,5},{5,4},{6,7},{7,6},{8,9},{9,8},{10,11... | collective-permute-start | bytes 393224 | tf_op jit(solution)/shard_map/ppermute | solution.py:336
  52.8 14.2 %collective-permute-start.11 = (bf16[1,8,32,128]{3,2,1,0:T(8,128)(2,1)}, bf16[1,8,32,128]{3,2,1,0:T(8,128)(2,1)S(1)}, u32[]{:S(2)}, u32[]{:S(2)}) collective-permute-start(bf16[1,8,32,128]{3,2,1,0:T(8,128)(2,1)} %get-tuple-element.64), channel_id=1, source_target_pairs={{0,4},{1,5},{2,6},{3,7},{4,0},{5,1},{6,2},{7,3},{8,12},{9,13},{10,... | collective-permute-start | bytes 196616 | tf_op jit(solution)/shard_map/ppermute | solution.py:336
  56.2 10.7 %collective-permute-start.7 = (bf16[1,8,32,128]{3,2,1,0:T(8,128)(2,1)S(1)}, bf16[1,8,32,128]{3,2,1,0:T(8,128)(2,1)S(1)}, u32[]{:S(2)}, u32[]{:S(2)}) collective-permute-start(bf16[1,8,32,128]{3,2,1,0:T(8,128)(2,1)S(1)} %slice.73), channel_id=1, source_target_pairs={{0,4},{1,5},{2,6},{3,7},{4,0},{5,1},{6,2},{7,3},{8,12},{9,13},{10,... | collective-permute-start | bytes 196616 | tf_op jit(solution)/shard_map/ppermute | solution.py:336
  56.8 10.1 %collective-permute-start.9 = (bf16[1,8,32,128]{3,2,1,0:T(8,128)(2,1)S(1)}, bf16[1,8,32,128]{3,2,1,0:T(8,128)(2,1)S(1)}, u32[]{:S(2)}, u32[]{:S(2)}) collective-permute-start(bf16[1,8,32,128]{3,2,1,0:T(8,128)(2,1)S(1)} %slice.77), channel_id=1, source_target_pairs={{0,4},{1,5},{2,6},{3,7},{4,0},{5,1},{6,2},{7,3},{8,12},{9,13},{10,... | collective-permute-start | bytes 196616 | tf_op jit(solution)/shard_map/ppermute | solution.py:336
  64.1 6.1 %collective-permute-start.13 = (bf16[1,8,32,128]{3,2,1,0:T(8,128)(2,1)}, bf16[1,8,32,128]{3,2,1,0:T(8,128)(2,1)S(1)}, u32[]{:S(2)}, u32[]{:S(2)}) collective-permute-start(bf16[1,8,32,128]{3,2,1,0:T(8,128)(2,1)} %get-tuple-element.68), channel_id=1, source_target_pairs={{0,4},{1,5},{2,6},{3,7},{4,0},{5,1},{6,2},{7,3},{8,12},{9,13},{10,... | collective-permute-start | bytes 196616 | tf_op jit(solution)/shard_map/ppermute | solution.py:336
  64.5 16.8 %collective-permute-start.21 = (bf16[16,32,128]{2,1,0:T(8,128)(2,1)}, bf16[16,32,128]{2,1,0:T(8,128)(2,1)S(1)}, u32[]{:S(2)}, u32[]{:S(2)}) collective-permute-start(bf16[16,32,128]{2,1,0:T(8,128)(2,1)} %get-tuple-element.77.refs_4_), channel_id=1, source_target_pairs={{0,16},{8,24},{16,0},{24,8},{1,17},{9,25},{17,1},{25,9},{2,18},{10... | collective-permute-start | bytes 393224 | tf_op jit(solution)/shard_map/ppermute | solution.py:539
  66.9 16.2 %copy-start = (bf16[16,32,128]{2,1,0:T(8,128)(2,1)}, bf16[16,32,128]{2,1,0:T(8,128)(2,1)S(1)}, u32[]{:S(2)}) copy-start(bf16[16,32,128]{2,1,0:T(8,128)(2,1)S(1)} %pad_maximum_fusion.refs_0_) | copy-start | bytes 393220
  70.1 11.7 %collective-permute-start.15 = (bf16[16,32,128]{2,1,0:T(8,128)(2,1)S(1)}, bf16[16,32,128]{2,1,0:T(8,128)(2,1)S(1)}, u32[]{:S(2)}, u32[]{:S(2)}) collective-permute-start(bf16[16,32,128]{2,1,0:T(8,128)(2,1)S(1)} %pad_maximum_fusion.refs_0_), channel_id=1, source_target_pairs={{0,8},{8,0},{16,24},{24,16},{1,9},{9,1},{17,25},{25,17},{2,10},{10... | collective-permute-start | bytes 393224 | tf_op jit(solution)/shard_map/ppermute | solution.py:539
  70.1 11.1 %collective-permute-start.14 = (bf16[16,32,128]{2,1,0:T(8,128)(2,1)S(1)}, bf16[16,32,128]{2,1,0:T(8,128)(2,1)S(1)}, u32[]{:S(2)}, u32[]{:S(2)}) collective-permute-start(bf16[16,32,128]{2,1,0:T(8,128)(2,1)S(1)} %pad_maximum_fusion.refs_0_), channel_id=1, source_target_pairs={{0,16},{8,24},{16,0},{24,8},{1,17},{9,25},{17,1},{25,9},{2,18},{10... | collective-permute-start | bytes 393224 | tf_op jit(solution)/shard_map/ppermute | solution.py:539
  73.3 7.5 %collective-permute-start.18 = (bf16[2,8,32,128]{3,2,1,0:T(8,128)(2,1)S(1)}, bf16[2,8,32,128]{3,2,1,0:T(8,128)(2,1)S(1)}, u32[]{:S(2)}, u32[]{:S(2)}) collective-permute-start(bf16[2,8,32,128]{3,2,1,0:T(8,128)(2,1)S(1)} %pad_maximum_fusion.2), channel_id=1, source_target_pairs={{0,1},{1,0},{2,3},{3,2},{4,5},{5,4},{6,7},{7,6},{8,9},{9,8},{10,11... | collective-permute-start | bytes 393224 | tf_op jit(solution)/shard_map/ppermute | solution.py:336
  74.9 5.3 %collective-permute-start.17 = (bf16[2,8,32,128]{3,2,1,0:T(8,128)(2,1)S(1)}, bf16[2,8,32,128]{3,2,1,0:T(8,128)(2,1)S(1)}, u32[]{:S(2)}, u32[]{:S(2)}) collective-permute-start(bf16[2,8,32,128]{3,2,1,0:T(8,128)(2,1)S(1)} %pad_maximum_fusion.1), channel_id=1, source_target_pairs={{0,2},{1,3},{2,0},{3,1},{4,6},{5,7},{6,4},{7,5},{8,10},{9,11},{10,... | collective-permute-start | bytes 393224 | tf_op jit(solution)/shard_map/ppermute | solution.py:336
  80.3 11.9 %copy-start.1 = (bf16[4,8,32,128]{3,2,1,0:T(8,128)(2,1)}, bf16[4,8,32,128]{3,2,1,0:T(8,128)(2,1)S(1)}, u32[]{:S(2)}) copy-start(bf16[4,8,32,128]{3,2,1,0:T(8,128)(2,1)S(1)} %constant_dynamic-update-slice_fusion.refs_0_) | copy-start | bytes 786436
  80.3 11.9 %collective-permute-start.19 = (bf16[4,8,32,128]{3,2,1,0:T(8,128)(2,1)S(1)}, bf16[4,8,32,128]{3,2,1,0:T(8,128)(2,1)S(1)}, u32[]{:S(2)}, u32[]{:S(2)}) collective-permute-start(bf16[4,8,32,128]{3,2,1,0:T(8,128)(2,1)S(1)} %constant_dynamic-update-slice_fusion.refs_0_), channel_id=1, source_target_pairs={{0,1},{1,0},{2,3},{3,2},{4,5},{5,4},{6,7},{7,6},{8,9},{9,8},{10,11... | collective-permute-start | bytes 786440 | tf_op jit(solution)/shard_map/ppermute | solution.py:336
  80.9 11.3 %copy-start.2 = (bf16[4,8,32,128]{3,2,1,0:T(8,128)(2,1)}, bf16[4,8,32,128]{3,2,1,0:T(8,128)(2,1)S(1)}, u32[]{:S(2)}) copy-start(bf16[4,8,32,128]{3,2,1,0:T(8,128)(2,1)S(1)} %constant_dynamic-update-slice_fusion.3.refs_2_) | copy-start | bytes 786436
  80.9 11.3 %collective-permute-start.20 = (bf16[4,8,32,128]{3,2,1,0:T(8,128)(2,1)S(1)}, bf16[4,8,32,128]{3,2,1,0:T(8,128)(2,1)S(1)}, u32[]{:S(2)}, u32[]{:S(2)}) collective-permute-start(bf16[4,8,32,128]{3,2,1,0:T(8,128)(2,1)S(1)} %constant_dynamic-update-slice_fusion.3.refs_2_), channel_id=1, source_target_pairs={{0,2},{1,3},{2,0},{3,1},{4,6},{5,7},{6,4},{7,5},{8,10},{9,11},{10,... | collective-permute-start | bytes 786440 | tf_op jit(solution)/shard_map/ppermute | solution.py:336
  81.3 1.9 %copy-start.9 = (bf16[16,32,128]{2,1,0:T(8,128)(2,1)}, bf16[16,32,128]{2,1,0:T(8,128)(2,1)S(1)}, u32[]{:S(2)}) copy-start(bf16[16,32,128]{2,1,0:T(8,128)(2,1)S(1)} %collective-permute-done.14.refs_1_) | copy-start | bytes 393220
  81.3 1.3 %collective-permute-start.16 = (bf16[16,32,128]{2,1,0:T(8,128)(2,1)S(1)}, bf16[16,32,128]{2,1,0:T(8,128)(2,1)S(1)}, u32[]{:S(2)}, u32[]{:S(2)}) collective-permute-start(bf16[16,32,128]{2,1,0:T(8,128)(2,1)S(1)} %collective-permute-done.14.refs_1_), channel_id=1, source_target_pairs={{0,8},{8,0},{16,24},{24,16},{1,9},{9,1},{17,25},{25,17},{2,10},{10... | collective-permute-start | bytes 393224 | tf_op jit(solution)/shard_map/ppermute | solution.py:539
  81.3 1.9 %copy-start.7 = (bf16[16,32,128]{2,1,0:T(8,128)(2,1)}, bf16[16,32,128]{2,1,0:T(8,128)(2,1)S(1)}, u32[]{:S(2)}) copy-start(bf16[16,32,128]{2,1,0:T(8,128)(2,1)S(1)} %collective-permute-done.21.refs_5_) | copy-start | bytes 393220
  81.3 1.7 %collective-permute-start.22 = (bf16[16,32,128]{2,1,0:T(8,128)(2,1)}, bf16[16,32,128]{2,1,0:T(8,128)(2,1)S(1)}, u32[]{:S(2)}, u32[]{:S(2)}) collective-permute-start(bf16[16,32,128]{2,1,0:T(8,128)(2,1)} %get-tuple-element.77.refs_4_), channel_id=1, source_target_pairs={{0,8},{8,0},{16,24},{24,16},{1,9},{9,1},{17,25},{25,17},{2,10},{10... | collective-permute-start | bytes 393224 | tf_op jit(solution)/shard_map/ppermute | solution.py:539
  81.8 1.4 %copy-start.8 = (bf16[16,32,128]{2,1,0:T(8,128)(2,1)}, bf16[16,32,128]{2,1,0:T(8,128)(2,1)S(1)}, u32[]{:S(2)}) copy-start(bf16[16,32,128]{2,1,0:T(8,128)(2,1)S(1)} %collective-permute-done.15.refs_2_) | copy-start | bytes 393220
  81.8 1.4 %collective-permute-start.23 = (bf16[16,32,128]{2,1,0:T(8,128)(2,1)S(1)}, bf16[16,32,128]{2,1,0:T(8,128)(2,1)S(1)}, u32[]{:S(2)}, u32[]{:S(2)}) collective-permute-start(bf16[16,32,128]{2,1,0:T(8,128)(2,1)S(1)} %collective-permute-done.21.refs_5_), channel_id=1, source_target_pairs={{0,8},{8,0},{16,24},{24,16},{1,9},{9,1},{17,25},{25,17},{2,10},{10... | collective-permute-start | bytes 393224 | tf_op jit(solution)/shard_map/ppermute | solution.py:539
  (7 other events, 4.6 us)
